TPU v7x, 32 devices: a 4x2x2 block of a 4x4x8 slice. The times are simulated.
32 devices in a mesh: dp: 4 (over y, z), tp: 8 (over x, core).
Axes of the slice: x: 4, y: 2, z: 2, core: 2. Of those that a mesh axis runs over, the one named last changes fastest.
The devices are a block of a 4x4x8 slice.
Arguments:
- hidden: bfloat16 [64, 256, 2560], P('dp', 'tp'), parts along dimension 0
- norm_gain: bfloat16 [2560], replicated
- w_dq: bfloat16 [2560, 768], replicated
- q_gain: bfloat16 [768], replicated
- w_dkv: bfloat16 [2560, 288], replicated
- kv_gain: bfloat16 [256], replicated
- w_uq: bfloat16 [768, 128, 64], P(None, 'tp')
- w_qr: bfloat16 [768, 128, 32], P(None, 'tp')
- w_uk: bfloat16 [256, 128, 64], P(None, 'tp')
- w_uv: bfloat16 [256, 128, 64], P(None, 'tp')
- w_out: bfloat16 [128, 64, 2560], P('tp')
- rope_cos: float32 [256, 16], replicated
- rope_sin: float32 [256, 16], replicated
- grad_out: bfloat16 [64, 256, 2560], P('dp', 'tp'), parts along dimension 0
Outputs:
- output 1: bfloat16 [64, 256, 2560], P('dp', 'tp'), parts along dimension 0
- output 2: float32 [64, 256, 2560], P('dp', 'tp'), parts along dimension 0
- output 3: float32 [10240], P('dp'), parts along dimension 0
- output 4: float32 [10240, 768], P('dp'), parts along dimension 0
- output 5: float32 [3072], P('dp'), parts along dimension 0
- output 6: float32 [10240, 288], P('dp'), parts along dimension 0
- output 7: float32 [1024], P('dp'), parts along dimension 0
- output 8: float32 [3072, 128, 64], P('dp', 'tp'), parts along dimension 0
- output 9: float32 [3072, 128, 32], P('dp', 'tp'), parts along dimension 0
- output 10: float32 [1024, 128, 64], P('dp', 'tp'), parts along dimension 0
- output 11: float32 [1024, 128, 64], P('dp', 'tp'), parts along dimension 0
- output 12: float32 [512, 64, 2560], P(('dp', 'tp')), parts along dimension 0
There are 4 independent parts. A program takes and returns all parts, laid end to end along the dimension named above; an argument that names none is the same for every part.
All inputs are finite; a program needn't handle non-finite values.
Results may differ from a plain program's by a relative error of at most 0.0171253.
Values are sent between devices in bfloat16 or wider.
A program may use at most 768 MiB of HBM per device.

v0:
```python
import jax
import jax.numpy as jnp
from jax import lax
from jax.sharding import PartitionSpec as P

NORM_EPS = 1e-6


def norm_forward(value, gain_vec):
    value32 = value.astype(jnp.float32)
    inv_rms = lax.rsqrt(jnp.mean(value32 * value32, axis=-1, keepdims=True) + NORM_EPS)
    unit_val = value32 * inv_rms
    return (unit_val * gain_vec.astype(jnp.float32)).astype(jnp.bfloat16), unit_val, inv_rms


def norm_backward(grad_norm, unit_val, inv_rms, gain_vec):
    grad_unit = grad_norm * gain_vec.astype(jnp.float32)
    grad_in = inv_rms * (grad_unit - unit_val * jnp.mean(grad_unit * unit_val, axis=-1, keepdims=True))
    grad_gain = jnp.sum(grad_norm * unit_val, axis=tuple(range(grad_norm.ndim - 1)))
    return grad_in, grad_gain


def rope_forward(value, cos_tab, sin_tab):
    half_dim = value.shape[-1] // 2
    lead_half = value[..., :half_dim].astype(jnp.float32)
    tail_half = value[..., half_dim:].astype(jnp.float32)
    rotated = jnp.concatenate([lead_half * cos_tab - tail_half * sin_tab, tail_half * cos_tab + lead_half * sin_tab], axis=-1)
    return rotated.astype(jnp.bfloat16)


def rope_backward(grad_rot, cos_tab, sin_tab):
    half_dim = grad_rot.shape[-1] // 2
    lead_grad = grad_rot[..., :half_dim]
    tail_grad = grad_rot[..., half_dim:]
    return jnp.concatenate([lead_grad * cos_tab + tail_grad * sin_tab, tail_grad * cos_tab - lead_grad * sin_tab], axis=-1)


def heads_forward(q_normed, kv_normed, k_rope, w_uq, w_qr, w_uk, w_uv, w_out, rope_cos, rope_sin):
    seq_len = q_normed.shape[1]
    score_scale = (w_uq.shape[2] + w_qr.shape[2]) ** -0.5
    q_nope = jnp.einsum('bsr,rhn->bshn', q_normed, w_uq, preferred_element_type=jnp.float32).astype(jnp.bfloat16)
    q_rope_in = jnp.einsum('bsr,rhn->bshn', q_normed, w_qr, preferred_element_type=jnp.float32).astype(jnp.bfloat16)
    q_rope = rope_forward(q_rope_in, rope_cos[:, None, :], rope_sin[:, None, :])
    k_nope = jnp.einsum('bsr,rhn->bshn', kv_normed, w_uk, preferred_element_type=jnp.float32).astype(jnp.bfloat16)
    values = jnp.einsum('bsr,rhv->bshv', kv_normed, w_uv, preferred_element_type=jnp.float32).astype(jnp.bfloat16)
    scores = (jnp.einsum('bqhn,bkhn->bhqk', q_nope, k_nope, preferred_element_type=jnp.float32) + jnp.einsum('bqhr,bkr->bhqk', q_rope, k_rope, preferred_element_type=jnp.float32)) * score_scale
    causal = jnp.arange(seq_len)[:, None] >= jnp.arange(seq_len)[None, :]
    attn_prob = jax.nn.softmax(jnp.where(causal, scores, -1e30), axis=-1)
    prob_bf = attn_prob.astype(jnp.bfloat16)
    head_out = jnp.einsum('bhqk,bkhv->bqhv', prob_bf, values, preferred_element_type=jnp.float32).astype(jnp.bfloat16)
    attn_part = jnp.einsum('criw,iwe->cre', head_out, w_out, preferred_element_type=jnp.float32).astype(jnp.bfloat16)
    return attn_part, (q_nope, q_rope, k_nope, values, attn_prob, prob_bf, head_out)


def heads_backward(grad_out_all, q_normed, kv_normed, k_rope, saved, w_uq, w_qr, w_uk, w_uv, w_out, rope_cos, rope_sin):
    q_nope, q_rope, k_nope, values, attn_prob, prob_bf, head_out = saved
    score_scale = (w_uq.shape[2] + w_qr.shape[2]) ** -0.5
    grad_w_out = jnp.einsum('criw,cre->iwe', head_out, grad_out_all, preferred_element_type=jnp.float32)
    grad_head = jnp.einsum('cre,iwe->criw', grad_out_all, w_out, preferred_element_type=jnp.float32).astype(jnp.bfloat16)
    grad_prob = jnp.einsum('bqhv,bkhv->bhqk', grad_head, values, preferred_element_type=jnp.float32)
    grad_values = jnp.einsum('bhqk,bqhv->bkhv', prob_bf, grad_head, preferred_element_type=jnp.float32).astype(jnp.bfloat16)
    grad_scores = (attn_prob * (grad_prob - jnp.sum(attn_prob * grad_prob, axis=-1, keepdims=True)) * score_scale).astype(jnp.bfloat16)
    grad_q_nope = jnp.einsum('bhqk,bkhn->bqhn', grad_scores, k_nope, preferred_element_type=jnp.float32).astype(jnp.bfloat16)
    grad_k_nope = jnp.einsum('bhqk,bqhn->bkhn', grad_scores, q_nope, preferred_element_type=jnp.float32).astype(jnp.bfloat16)
    grad_q_rope = jnp.einsum('bhqk,bkr->bqhr', grad_scores, k_rope, preferred_element_type=jnp.float32)
    grad_k_rope = jnp.einsum('bhqk,bqhr->bkr', grad_scores, q_rope, preferred_element_type=jnp.float32)
    grad_q_rope_in = rope_backward(grad_q_rope, rope_cos[:, None, :], rope_sin[:, None, :]).astype(jnp.bfloat16)
    grad_k_rope_in = rope_backward(grad_k_rope, rope_cos, rope_sin)
    grad_w_uq = jnp.einsum('bsr,bshn->rhn', q_normed, grad_q_nope, preferred_element_type=jnp.float32)
    grad_w_qr = jnp.einsum('bsr,bshn->rhn', q_normed, grad_q_rope_in, preferred_element_type=jnp.float32)
    grad_w_uk = jnp.einsum('bsr,bshn->rhn', kv_normed, grad_k_nope, preferred_element_type=jnp.float32)
    grad_w_uv = jnp.einsum('bsr,bshv->rhv', kv_normed, grad_values, preferred_element_type=jnp.float32)
    grad_q_normed = jnp.einsum('bshn,rhn->bsr', grad_q_nope, w_uq, preferred_element_type=jnp.float32) + jnp.einsum('bshn,rhn->bsr', grad_q_rope_in, w_qr, preferred_element_type=jnp.float32)
    grad_kv_normed = jnp.einsum('bshn,rhn->bsr', grad_k_nope, w_uk, preferred_element_type=jnp.float32) + jnp.einsum('bshv,rhv->bsr', grad_values, w_uv, preferred_element_type=jnp.float32)
    return grad_q_normed, grad_kv_normed, grad_k_rope_in, (grad_w_uq, grad_w_qr, grad_w_uk, grad_w_uv, grad_w_out)


def solution(mesh):
    act_spec = P('dp', 'tp', None)
    head_spec = P(None, 'tp', None)
    in_specs = (act_spec, P(None), P(None, None), P(None), P(None, None), P(None), head_spec, head_spec, head_spec, head_spec, P('tp', None, None), P(None, None), P(None, None), act_spec)
    grad_head_spec = P('dp', 'tp', None)
    out_specs = (act_spec, act_spec, P('dp'), P('dp', None), P('dp'), P('dp', None), P('dp'), grad_head_spec, grad_head_spec, grad_head_spec, grad_head_spec, P(('dp', 'tp'), None, None))

    def local_step(hidden, norm_gain, w_dq, q_gain, w_dkv, kv_gain, w_uq, w_qr, w_uk, w_uv, w_out, rope_cos, rope_sin, grad_out):
        kv_rank = kv_gain.shape[0]
        normed, x_unit, x_inv = norm_forward(hidden, norm_gain)
        normed_all = lax.all_gather(normed, 'tp', axis=1, tiled=True)
        q_latent = jnp.einsum('bsd,dr->bsr', normed_all, w_dq, preferred_element_type=jnp.float32).astype(jnp.bfloat16)
        kv_latent = jnp.einsum('bsd,dr->bsr', normed_all, w_dkv, preferred_element_type=jnp.float32).astype(jnp.bfloat16)
        q_normed, q_unit, q_inv = norm_forward(q_latent, q_gain)
        kv_normed, kv_unit, kv_inv = norm_forward(kv_latent[:, :, :kv_rank], kv_gain)
        k_rope = rope_forward(kv_latent[:, :, kv_rank:], rope_cos, rope_sin)
        attn_part, saved = heads_forward(q_normed, kv_normed, k_rope, w_uq, w_qr, w_uk, w_uv, w_out, rope_cos, rope_sin)
        attn_out = lax.psum_scatter(attn_part, 'tp', scatter_dimension=1, tiled=True)
        out_hidden = (hidden.astype(jnp.float32) + attn_out.astype(jnp.float32)).astype(jnp.bfloat16)

        grad_out_all = lax.all_gather(grad_out, 'tp', axis=1, tiled=True)
        grad_q_normed, grad_kv_normed, grad_k_rope_in, head_grads = heads_backward(grad_out_all, q_normed, kv_normed, k_rope, saved, w_uq, w_qr, w_uk, w_uv, w_out, rope_cos, rope_sin)
        grad_q_latent, grad_q_gain = norm_backward(grad_q_normed, q_unit, q_inv, q_gain)
        grad_kv_nope, grad_kv_gain = norm_backward(grad_kv_normed, kv_unit, kv_inv, kv_gain)
        grad_q_latent = grad_q_latent.astype(jnp.bfloat16)
        grad_kv_latent = jnp.concatenate([grad_kv_nope, grad_k_rope_in], axis=-1).astype(jnp.bfloat16)
        grad_w_dq = jnp.einsum('bsd,bsr->dr', normed_all, grad_q_latent, preferred_element_type=jnp.float32)
        grad_w_dkv = jnp.einsum('bsd,bsr->dr', normed_all, grad_kv_latent, preferred_element_type=jnp.float32)
        grad_normed_part = (jnp.einsum('bsr,dr->bsd', grad_q_latent, w_dq, preferred_element_type=jnp.float32) + jnp.einsum('bsr,dr->bsd', grad_kv_latent, w_dkv, preferred_element_type=jnp.float32)).astype(jnp.bfloat16)
        grad_normed = lax.psum_scatter(grad_normed_part, 'tp', scatter_dimension=1, tiled=True)
        grad_x_norm, grad_norm_gain = norm_backward(grad_normed.astype(jnp.float32), x_unit, x_inv, norm_gain)
        grad_hidden = grad_out.astype(jnp.float32) + grad_x_norm
        summed = lax.psum((grad_norm_gain, grad_w_dq, grad_q_gain, grad_w_dkv, grad_kv_gain), 'tp')
        return (out_hidden, grad_hidden) + tuple(summed) + tuple(head_grads)

    return jax.shard_map(local_step, mesh=mesh, in_specs=in_specs, out_specs=out_specs, check_vma=False)
```

profile of v0, /device:TPU:81, one launch (start us, length us, event | category | flops | bytes accessed | tf_op | source)
XLA Modules:
  0.0 1195.3 jit_solution(9835667600332140607)
XLA Ops:
  7.2 0.0 copy-start
  7.2 0.1 all-gather.3.cloned.1.call-start
  7.3 2.4 fusion.87
  9.7 0.7 convert_element_type.120
  10.4 0.6 copy-done.33
  11.0 3.9 fusion.84
  14.9 0.1 all-gather.3.cloned.1.call-update
  15.0 0.1 all-gather.5.cloned.1.call-start
  15.1 0.7 all-gather.5.cloned.1.call-update
  15.8 0.1 reduce-scatter.5.cloned.1.call-start
  15.9 0.7 iota_compare_fusion
  16.6 103.0 %all-gather.3.cloned.1.call-done = bf16[16,256,2560]{2,1,0:T(8,128)(2,1)} async-done(((bf16[16,32,2560]{2,1,0:T(8,128)(2,1)}), bf16[16,256,2560]{2,1,0:T(8,128)(2,1)}) %all-gather.3.cloned.1.call-update) | async-done | bytes 20971536 | tf_op jit(solution)/shard_map/all_gather | solution.py:88
  119.6 20.9 %fusion.37 = (f32[16,256]{1,0:T(8,128)S(1)}, bf16[16,256,768]{2,1,0:T(8,128)(2,1)S(1)}) fusion(bf16[16,256,2560]{2,1,0:T(8,128)(2,1)} %all-gather.3.cloned.1.call-done, bf16[2560,768]{1,0:T(8,128)(2,1)} %param.16), kind=kOutput, calls=%fused_computation.36 | convolution fusion | flops 16118706176 | bytes 31211520 | tf_op jit(solution)/shard_map/bsd,dr->bsr/dot_general | solution.py:89
  140.6 13.0 %convolution_convert_fusion.4 = bf16[16,256,288]{1,2,0:T(8,128)(2,1)S(1)} fusion(bf16[16,256,2560]{2,1,0:T(8,128)(2,1)} %all-gather.3.cloned.1.call-done, bf16[2560,288]{0,1:T(8,128)(2,1)S(1)} %copy-done.21), kind=kOutput, calls=%fused_computation.118 | convolution fusion | flops 6040977408 | bytes 24805376 | tf_op jit(solution)/shard_map/bsd,dr->bsr/dot_general | solution.py:90
  153.6 0.4 fusion.97
  154.1 0.1 fusion.141
  154.2 3.9 convolution_convert_fusion.3
  158.1 3.3 fusion.99
  161.4 5.7 convolution_convert_fusion.2
  167.1 9.4 convolution_convert_fusion.1
  176.5 45.4 %all-gather.5.cloned.1.call-done = bf16[16,256,2560]{2,1,0:T(8,128)(2,1)} async-done(((bf16[16,32,2560]{2,1,0:T(8,128)(2,1)}), bf16[16,256,2560]{2,1,0:T(8,128)(2,1)}) %all-gather.5.cloned.1.call-update) | async-done | bytes 20971536 | tf_op jit(solution)/shard_map/all_gather | solution.py:98
  221.8 27.8 %fusion.68 = bf16[16,256,16,64]{1,3,2,0:T(8,128)(2,1)} fusion(bf16[16,256,2560]{2,1,0:T(8,128)(2,1)} %all-gather.5.cloned.1.call-done, bf16[16,64,2560]{2,1,0:T(8,128)(2,1)} %param.24), kind=kOutput, calls=%fused_computation.66 | convolution fusion | flops 21479030784 | bytes 34603008 | tf_op jit(solution)/shard_map/cre,iwe->criw/dot_general | solution.py:59
  249.6 29.5 %fusion.176 = f32[16,16,256,256]{2,3,1,0:T(8,128)} fusion(bf16[16,256,16,64]{1,3,2,0:T(8,128)(2,1)} %fusion.68, bf16[16,256,16,64]{1,3,2,0:T(8,128)(2,1)} %convolution_convert_fusion.2), kind=kOutput, calls=%fused_computation.169 | convolution fusion | flops 2147483648 | bytes 83886080 | tf_op jit(solution)/shard_map/bqhv,bkhv->bhqk/dot_general | solution.py:60
  279.1 25.4 %fusion.112 = f32[16,256,256,16]{2,1,3,0:T(8,128)} fusion(bf16[16,256,16,16]{1,3,2,0:T(8,128)(2,1)} %get-tuple-element.26, bf16[16,256,16,16]{1,3,2,0:T(8,128)(2,1)} %get-tuple-element.25, bf16[16,256,16]{1,2,0:T(8,128)(2,1)S(1)} %get-tuple-element.30, bf16[16,256,16]{1,2,0:T(8,128)(2,1)S(1)} %get-tuple-element.29), kind=kOutput, calls=%fused_computation.114 | convolution fusion | flops 1082654720 | bytes 71565312 | tf_op jit(solution)/shard_map/bqhr,bkr->bhqk/dot_general | solution.py:46
  304.6 54.4 %fusion.167 = (f32[16,16,256]{2,1,0:T(8,128)S(1)}, f32[16,16,256,256]{2,3,1,0:T(8,128)}) fusion(f32[16,256,256,16]{2,1,3,0:T(8,128)} %fusion.112, pred[256,256]{0,1:T(8,128)(4,1)S(1)} %copy-done.12, bf16[16,256,16,64]{1,3,2,0:T(8,128)(2,1)} %convolution_convert_fusion.1, bf16[256,16,64]{0,2,1:T(8,128)(2,1)S(1)} %copy-done.6, ...), kind=kOutput, calls=%fused_computation.168 | convolution fusion | flops 4387241984 | bytes 145572864 | tf_op jit(solution)/shard_map/sub | solution.py:48
  359.0 84.0 %fusion.108 = f32[16,256,16,32]{1,3,2,0:T(8,128)} fusion(f32[16,16,256,256]{2,3,1,0:T(8,128)} %fusion.176, bf16[16,256,16]{1,2,0:T(8,128)(2,1)S(1)} %get-tuple-element.30, bf16[16,256,16]{1,2,0:T(8,128)(2,1)S(1)} %get-tuple-element.29, f32[16,16,256,256]{2,3,1,0:T(8,128)} %get-tuple-element.36, f32[16,16,256]{2,1,0:T(8,128)S(1)} %get-tuple-element.35), kind=kOutput, calls=%fused_computation.112 | convolution fusion | flops 1191772416 | bytes 143130624 | tf_op jit(solution)/shard_map/bhqk,bkr->bqhr/dot_general | solution.py:65
  442.9 85.3 %fusion.59 = bf16[16,16,64,256]{3,2,1,0:T(8,128)(2,1)} fusion(bf16[16,256,16,64]{1,3,2,0:T(8,128)(2,1)} %convolution_convert_fusion.1, f32[16,16,256,256]{2,3,1,0:T(8,128)} %fusion.176, f32[16,16,256,256]{2,3,1,0:T(8,128)} %get-tuple-element.36, f32[16,16,256]{2,1,0:T(8,128)S(1)} %get-tuple-element.35), kind=kOutput, calls=%fused_computation.60 | convolution fusion | flops 2269184256 | bytes 151257088 | tf_op jit(solution)/shard_map/bhqk,bqhn->bkhn/dot_general | solution.py:64
  528.3 28.5 %fusion.65 = bf16[16,16,64,256]{3,2,1,0:T(8,128)(2,1)} fusion(bf16[16,256,16,64]{1,3,2,0:T(8,128)(2,1)} %fusion.68, f32[16,16,256,256]{2,3,1,0:T(8,128)} %get-tuple-element.36, f32[16,16,256]{2,1,0:T(8,128)S(1)} %get-tuple-element.35), kind=kOutput, calls=%fused_computation.65 | convolution fusion | flops 2185232384 | bytes 84148224 | tf_op jit(solution)/shard_map/bhqk,bqhv->bkhv/dot_general | solution.py:61
  556.8 83.1 %fusion.131 = f32[16,256,32]{1,2,0:T(8,128)S(1)} fusion(bf16[16,256,16,16]{1,3,2,0:T(8,128)(2,1)} %get-tuple-element.26, bf16[16,256,16,16]{1,3,2,0:T(8,128)(2,1)} %get-tuple-element.25, f32[16,16,256,256]{2,3,1,0:T(8,128)} %fusion.176, f32[16,16,256,256]{2,3,1,0:T(8,128)} %get-tuple-element.36, f32[16,16,256]{2,1,0:T(8,128)S(1)} %get-tuple-element.35), kind=kOutput, calls=%fused_computation.128 | convolution fusion | flops 1199636736 | bytes 139198464 | tf_op jit(solution)/shard_map/bhqk,bqhr->bkr/dot_general | solution.py:66
  640.0 7.6 convolution_convert_fusion
  647.6 3.5 add_convert_fusion.1
  651.1 1.6 copy-done.52
  652.7 2.5 fusion.40
  655.1 9.4 fusion.96
  664.5 0.8 add_convert_fusion.2
  665.3 86.7 %fusion.56 = bf16[16,16,64,256]{3,2,1,0:T(8,128)(2,1)} fusion(bf16[16,256,16,64]{1,3,2,0:T(8,128)(2,1)} %convolution_convert_fusion, f32[16,16,256,256]{2,3,1,0:T(8,128)} %fusion.176, f32[16,16,256,256]{2,3,1,0:T(8,128)} %get-tuple-element.36, f32[16,16,256]{2,1,0:T(8,128)S(1)} %get-tuple-element.35), kind=kOutput, calls=%fused_computation.59 | convolution fusion | flops 2269184256 | bytes 151257088 | tf_op jit(solution)/shard_map/bhqk,bkhn->bqhn/dot_general | solution.py:63
  752.0 13.0 %fusion.48 = f32[16,256,768,1]{2,1,3,0:T(8,128)} fusion(bf16[16,16,64,256]{3,2,1,0:T(8,128)(2,1)} %fusion.56, bf16[768,16,64]{0,2,1:T(8,128)(2,1)S(1)} %copy-done), kind=kOutput, calls=%fused_computation.48 | convolution fusion | flops 6442450944 | bytes 22544384 | tf_op jit(solution)/shard_map/bshn,rhn->bsr/dot_general | solution.py:73
  765.1 13.3 %fusion.36 = (f32[768]{0:T(1024)}, f32[16,256]{1,0:T(8,128)S(1)}, f32[16,256,768]{2,1,0:T(8,128)}) fusion(bf16[16,256,768]{2,1,0:T(8,128)(2,1)} %copy-done.11, f32[16,256]{1,0:T(8,128)S(1)} %copy-done.41, f32[768]{0:T(1024)S(1)} %copy-done.44, bf16[768,16,32]{0,2,1:T(8,128)(2,1)S(1)} %copy-done.50, bf16[16,256,16,16]{1,3,2,0:T(8,128)(2,1)} %get-tuple-element.24, ...), kind=kOutput, calls=%fused_computation.35 | convolution fusion | flops 3254775040 | bytes 36476928 | tf_op jit(solution)/shard_map/bshn,rhn->bsr/dot_general | solution.py:73
  778.4 0.9 fusion.95
  779.4 10.8 fusion.35
  790.3 17.0 %fusion.122 = f32[16,256,2560]{2,1,0:T(8,128)} fusion(bf16[2560,288]{0,1:T(8,128)(2,1)S(1)} %copy-done.22, bf16[16,256,16]{1,2,0:T(8,128)(2,1)S(1)} %copy-done.25, bf16[16,256,16]{1,2,0:T(8,128)(2,1)S(1)} %copy-done.23, bf16[16,256,256]{1,2,0:T(8,128)(2,1)S(1)} %fusion.95), kind=kOutput, calls=%fused_computation.123 | convolution fusion | flops 6046875648 | bytes 45776896 | tf_op jit(solution)/shard_map/bsr,dr->bsd/dot_general | solution.py:106
  807.3 29.4 %add_convert_fusion = bf16[16,256,2560]{2,1,0:T(8,128)(2,1)} fusion(f32[16,256,2560]{2,1,0:T(8,128)} %fusion.122, bf16[16,256,768]{2,1,0:T(8,128)(2,1)} %fusion.35, bf16[2560,768]{1,0:T(8,128)(2,1)} %param.16), kind=kOutput, calls=%fused_computation.10 | convolution fusion | flops 16127098880 | bytes 73138176 | tf_op jit(solution)/shard_map/bsr,dr->bsd/dot_general | solution.py:106
  836.7 0.1 reduce-scatter.5.cloned.1.call-update
  836.8 0.1 reduce-scatter.3.cloned.1.call-start
  836.8 27.7 %fusion.62 = bf16[16,16,64,256]{3,2,1,0:T(8,128)(2,1)} fusion(bf16[16,256,16,64]{1,3,2,0:T(8,128)(2,1)} %convolution_convert_fusion.2, f32[16,16,256,256]{2,3,1,0:T(8,128)} %get-tuple-element.36, f32[16,16,256]{2,1,0:T(8,128)S(1)} %get-tuple-element.35), kind=kOutput, calls=%fused_computation.64 | convolution fusion | flops 2185232384 | bytes 84148224 | tf_op jit(solution)/shard_map/bhqk,bkhv->bqhv/dot_general | solution.py:50
  864.5 28.1 %bitcast_convert_fusion = bf16[16,256,2560]{2,1,0:T(8,128)(2,1)} fusion(bf16[16,16,64,256]{3,2,1,0:T(8,128)(2,1)} %fusion.62, bf16[16,64,2560]{2,1,0:T(8,128)(2,1)} %param.24), kind=kOutput, calls=%fused_computation.9 | convolution fusion | flops 21485322240 | bytes 34603008 | tf_op jit(solution)/shard_map/criw,iwe->cre/dot_general | solution.py:51
  892.6 0.1 reduce-scatter.3.cloned.1.call-update
  892.7 0.1 all-reduce.4.cloned.1.call-start
  892.8 0.6 copy-done.17
  893.3 7.6 fusion.125
  901.0 3.4 fusion.128
  904.4 12.3 %convolution_bitcast_fusion.1 = f32[2560,288]{0,1:T(8,128)} fusion(bf16[16,256,2560]{2,1,0:T(8,128)(2,1)} %all-gather.3.cloned.1.call-done, bf16[16,256,16]{1,2,0:T(8,128)(2,1)S(1)} %copy-done.26, bf16[16,256,16]{1,2,0:T(8,128)(2,1)S(1)} %copy-done.24, bf16[16,256,256]{1,2,0:T(8,128)(2,1)S(1)} %copy-done.10), kind=kOutput, calls=%fused_computation.91 | convolution fusion | flops 6046875648 | bytes 26279936 | tf_op jit(solution)/shard_map/bsd,bsr->dr/dot_general | solution.py:105
  916.7 21.6 %convolution_bitcast_fusion = f32[2560,768]{1,0:T(8,128)} fusion(bf16[16,256,2560]{2,1,0:T(8,128)(2,1)} %all-gather.3.cloned.1.call-done, bf16[16,256,768]{2,1,0:T(8,128)(2,1)S(1)} %bitcast.197), kind=kOutput, calls=%fused_computation.71 | convolution fusion | flops 16106127360 | bytes 35127296 | tf_op jit(solution)/shard_map/bsd,bsr->dr/dot_general | solution.py:104
  938.3 14.7 %fusion.116 = f32[768,16,64]{0,2,1:T(8,128)} fusion(bf16[16,16,64,256]{3,2,1,0:T(8,128)(2,1)} %fusion.56, bf16[16,256,768]{2,1,0:T(8,128)(2,1)} %copy-done.11, f32[768]{0:T(1024)S(1)} %copy-done.45, f32[16,256]{1,0:T(8,128)S(1)} %copy-done.42), kind=kOutput, calls=%fused_computation.119 | convolution fusion | flops 6455033856 | bytes 17845248 | tf_op jit(solution)/shard_map/bsr,bshn->rhn/dot_general | solution.py:69
  953.0 0.1 all-reduce.4.cloned.1.call-update
  953.1 33.4 %fusion.71 = f32[16,64,2560]{2,1,0:T(8,128)} fusion(bf16[16,256,2560]{2,1,0:T(8,128)(2,1)} %all-gather.5.cloned.1.call-done, bf16[16,16,64,256]{3,2,1,0:T(8,128)(2,1)} %fusion.62), kind=kOutput, calls=%fused_computation.68 | convolution fusion | flops 21474836480 | bytes 39845888 | tf_op jit(solution)/shard_map/criw,cre->iwe/dot_general | solution.py:58
  986.5 7.6 fusion.121
  994.2 4.5 fusion.86
  998.7 22.2 %all-reduce = (f32[2560]{0:T(1024)}, f32[768]{0:T(1024)}, f32[256]{0:T(256)}) all-reduce(f32[2560]{0:T(1024)S(1)} %get-tuple-element.16, f32[768]{0:T(1024)S(1)} %copy-done.46, f32[256]{0:T(256)S(1)} %copy-done.48), channel_id=1, replica_groups=mesh['dp'=4,'tp'=8] {'tp'}, use_global_device_ids=true, to_apply=%region_12.13 | all-reduce | flops 3584 | bytes 28672 | tf_op jit(solution)/shard_map/psum | solution.py:110
  1020.9 35.1 %reduce-scatter.3.cloned.1.call-done = bf16[16,32,2560]{2,1,0:T(8,128)(2,1)} async-done(((bf16[16,256,2560]{2,1,0:T(8,128)(2,1)}), bf16[16,32,2560]{2,1,0:T(8,128)(2,1)}) %reduce-scatter.3.cloned.1.call-update) | async-done | bytes 2621456 | tf_op jit(solution)/shard_map/reduce_scatter | solution.py:95
  1056.0 7.2 fusion.83
  1063.2 116.4 %all-reduce.4.cloned.1.call-done = (f32[2560,768]{1,0:T(8,128)}, f32[2560,288]{0,1:T(8,128)}) async-done(((f32[2560,768]{1,0:T(8,128)}, f32[2560,288]{0,1:T(8,128)}), (f32[2560,768]{1,0:T(8,128)}, f32[2560,288]{0,1:T(8,128)})) %all-reduce.4.cloned.1.call-update) | async-done | bytes 10813456 | tf_op jit(solution)/shard_map/psum | solution.py:110
  1179.6 7.1 copy.73
  1186.7 1.6 copy.74
  (118 shorter events, 0.3 us)
Async XLA Ops:
  7.2 159.9 %copy-start = (bf16[768,16,64]{0,2,1:T(8,128)(2,1)S(1)}, bf16[768,16,64]{0,2,1:T(8,128)(2,1)}, u32[]{:S(2)}) copy-start(bf16[768,16,64]{0,2,1:T(8,128)(2,1)} %param.20) | copy-start | bytes 4718596
  7.2 8.7 copy-start.47
  7.2 8.7 copy-start.51
  7.2 112.4 %all-gather.3.cloned.1.call-start = ((), (), s32[]{:S(2)}) async-start(), calls=%async_computation.2 | async-start | bytes 23592960 | tf_op jit(solution)/shard_map/all_gather | solution.py:88
  9.7 0.7 copy-start.35
  10.4 0.6 copy-start.33
  15.0 206.8 %all-gather.5.cloned.1.call-start = ((), (), s32[]{:S(2)}) async-start(), calls=%async_computation.4 | async-start | bytes 23592960 | tf_op jit(solution)/shard_map/all_gather | solution.py:98
  15.8 978.4 %reduce-scatter.5.cloned.1.call-start = ((), (), s32[]{:S(2)}) async-start(), calls=%async_computation.5 | async-start | bytes 23592960 | tf_op jit(solution)/shard_map/reduce_scatter | solution.py:107
  15.9 151.2 %copy-start.43 = (f32[768]{0:T(1024)}, f32[768]{0:T(1024)S(1)}, u32[]{:S(2)}) copy-start(f32[768]{0:T(1024)S(1)} %convert_element_type.129) | copy-start | bytes 9220
  15.9 288.6 %copy-start.37 = (f32[256]{0:T(256)}, f32[256]{0:T(256)S(1)}, u32[]{:S(2)}) copy-start(f32[256]{0:T(256)S(1)} %convert_element_type.124) | copy-start | bytes 3076
  16.6 123.9 %copy-start.21 = (bf16[2560,288]{0,1:T(8,128)(2,1)S(1)}, bf16[2560,288]{0,1:T(8,128)(2,1)}, u32[]{:S(2)}) copy-start(bf16[2560,288]{0,1:T(8,128)(2,1)} %param.18) | copy-start | bytes 4423684
  140.5 26.6 %copy-start.11 = (bf16[16,256,768]{2,1,0:T(8,128)(2,1)}, bf16[16,256,768]{2,1,0:T(8,128)(2,1)S(1)}, u32[]{:S(2)}) copy-start(bf16[16,256,768]{2,1,0:T(8,128)(2,1)S(1)} %get-tuple-element.34) | copy-start | bytes 18874372
  140.6 26.5 %copy-start.40 = (f32[16,256]{1,0:T(8,128)}, f32[16,256]{1,0:T(8,128)S(1)}, u32[]{:S(2)}) copy-start(f32[16,256]{1,0:T(8,128)S(1)} %add_rsqrt_fusion) | copy-start | bytes 49156
  140.6 13.5 %copy-start.29 = (f32[256,16]{0,1:T(8,128)S(1)}, f32[256,16]{0,1:T(8,128)}, u32[]{:S(2)}) copy-start(f32[256,16]{0,1:T(8,128)} %param.26) | copy-start | bytes 49156
  140.6 13.5 %copy-start.31 = (f32[256,16]{0,1:T(8,128)S(1)}, f32[256,16]{0,1:T(8,128)}, u32[]{:S(2)}) copy-start(f32[256,16]{0,1:T(8,128)} %param.25) | copy-start | bytes 49156
  140.6 13.6 %copy-start.49 = (bf16[768,16,32]{0,2,1:T(8,128)(2,1)S(1)}, bf16[768,16,32]{0,2,1:T(8,128)(2,1)}, u32[]{:S(2)}) copy-start(bf16[768,16,32]{0,2,1:T(8,128)(2,1)} %param.21) | copy-start | bytes 2359300
  153.6 7.7 copy-start.2
  154.1 150.4 %copy-start.15 = (f32[16,256]{1,0:T(8,128)}, f32[16,256]{1,0:T(8,128)S(1)}, u32[]{:S(2)}) copy-start(f32[16,256]{1,0:T(8,128)S(1)} %add_rsqrt_fusion.1) | copy-start | bytes 49156
  158.1 3.3 copy-start.27
  279.1 25.5 %copy-start.6 = (bf16[256,16,64]{0,2,1:T(8,128)(2,1)S(1)}, bf16[256,16,64]{0,2,1:T(8,128)(2,1)}, u32[]{:S(2)}) copy-start(bf16[256,16,64]{0,2,1:T(8,128)(2,1)} %param.22) | copy-start | bytes 1572868
  279.1 25.5 %copy-start.12 = (pred[256,256]{0,1:T(8,128)(4,1)S(1)}, pred[256,256]{0,1:T(8,128)(4,1)}, u32[]{:S(2)}) copy-start(pred[256,256]{0,1:T(8,128)(4,1)} %iota_compare_fusion) | copy-start | bytes 196612
  556.8 83.1 %copy-start.7 = (bf16[256,16,64]{0,2,1:T(8,128)(2,1)S(1)}, bf16[256,16,64]{0,2,1:T(8,128)(2,1)}, u32[]{:S(2)}) copy-start(bf16[256,16,64]{0,2,1:T(8,128)(2,1)} %param.22) | copy-start | bytes 1572868
  556.8 83.1 %copy-start.16 = (f32[16,256]{1,0:T(8,128)S(1)}, f32[16,256]{1,0:T(8,128)}, u32[]{:S(2)}) copy-start(f32[16,256]{1,0:T(8,128)} %copy-done.15) | copy-start | bytes 49156
  556.8 83.1 %copy-start.38 = (f32[256]{0:T(256)S(1)}, f32[256]{0:T(256)}, u32[]{:S(2)}) copy-start(f32[256]{0:T(256)} %copy-done.37) | copy-start | bytes 3076
  639.9 7.6 copy-start.8
  639.9 7.6 copy-start.30
  640.0 7.6 copy-start.32
  647.6 3.5 copy-start.28
  647.6 5.1 copy-start.52
  652.7 2.5 copy-start.3
  752.0 13.0 %copy-start.18 = (bf16[16,256,16,16]{1,3,2,0:T(8,128)(2,1)S(1)}, bf16[16,256,16,16]{1,3,2,0:T(8,128)(2,1)}, u32[]{:S(2)}) copy-start(bf16[16,256,16,16]{1,3,2,0:T(8,128)(2,1)} %get-tuple-element.23) | copy-start | bytes 6291460
  752.0 13.0 %copy-start.41 = (f32[16,256]{1,0:T(8,128)S(1)}, f32[16,256]{1,0:T(8,128)}, u32[]{:S(2)}) copy-start(f32[16,256]{1,0:T(8,128)} %copy-done.40) | copy-start | bytes 49156
  752.0 13.0 %copy-start.44 = (f32[768]{0:T(1024)S(1)}, f32[768]{0:T(1024)}, u32[]{:S(2)}) copy-start(f32[768]{0:T(1024)} %copy-done.43) | copy-start | bytes 9220
  752.0 13.0 %copy-start.50 = (bf16[768,16,32]{0,2,1:T(8,128)(2,1)S(1)}, bf16[768,16,32]{0,2,1:T(8,128)(2,1)}, u32[]{:S(2)}) copy-start(bf16[768,16,32]{0,2,1:T(8,128)(2,1)} %param.21) | copy-start | bytes 2359300
  765.1 13.3 %copy-start.4 = (bf16[16,256,288]{1,2,0:T(8,128)(2,1)S(1)}, bf16[16,256,288]{1,2,0:T(8,128)(2,1)}, u32[]{:S(2)}) copy-start(bf16[16,256,288]{1,2,0:T(8,128)(2,1)} %copy-done.2) | copy-start | bytes 7077892
  765.1 13.3 %copy-start.13 = (f32[16,256,256]{1,2,0:T(8,128)S(1)}, f32[16,256,256]{1,2,0:T(8,128)}, u32[]{:S(2)}) copy-start(f32[16,256,256]{1,2,0:T(8,128)} %get-tuple-element.37) | copy-start | bytes 12582916
  779.3 10.9 copy-start.9
  779.4 10.9 copy-start.22
  779.4 10.9 copy-start.23
  779.4 10.9 copy-start.25
  836.8 219.3 %reduce-scatter.3.cloned.1.call-start = ((), (), s32[]{:S(2)}) async-start(), calls=%async_computation.3 | async-start | bytes 23592960 | tf_op jit(solution)/shard_map/reduce_scatter | solution.py:95
  892.6 0.7 copy-start.17
  892.6 0.7 copy-start.39
  892.7 286.9 %all-reduce.4.cloned.1.call-start = ((), (), s32[]{:S(2)}) async-start(), calls=%async_computation.6 | async-start | bytes 21626880 | tf_op jit(solution)/shard_map/psum | solution.py:110
  893.3 7.6 copy-start.5
  893.3 7.6 copy-start.53
  900.9 3.5 copy-start.10
  900.9 3.5 copy-start.24
  900.9 3.4 copy-start.26
  901.0 15.8 %slice-start = ((s8[6291456]{0:T(1024)(128)(4,1)}), s8[4194304]{0:T(1024)(128)(4,1)S(1)}, s32[]{:S(2)}) async-start(s8[6291456]{0:T(1024)(128)(4,1)} %bitcast.196), calls=%async_computation.7 | async-start | bytes 8388608
  904.4 12.3 %slice-start.1 = ((s8[6291456]{0:T(1024)(128)(4,1)}), s8[2097152]{0:T(1024)(128)(4,1)S(1)}, s32[]{:S(2)}) async-start(s8[6291456]{0:T(1024)(128)(4,1)} %bitcast.196), calls=%async_computation.8 | async-start | bytes 4194304
  916.7 21.6 %copy-start.42 = (f32[16,256]{1,0:T(8,128)S(1)}, f32[16,256]{1,0:T(8,128)}, u32[]{:S(2)}) copy-start(f32[16,256]{1,0:T(8,128)} %copy-done.40) | copy-start | bytes 49156
  916.7 21.6 %copy-start.45 = (f32[768]{0:T(1024)S(1)}, f32[768]{0:T(1024)}, u32[]{:S(2)}) copy-start(f32[768]{0:T(1024)} %copy-done.43) | copy-start | bytes 9220
  953.0 33.5 %copy-start.19 = (bf16[16,256,16,16]{1,3,2,0:T(8,128)(2,1)S(1)}, bf16[16,256,16,16]{1,3,2,0:T(8,128)(2,1)}, u32[]{:S(2)}) copy-start(bf16[16,256,16,16]{1,3,2,0:T(8,128)(2,1)} %get-tuple-element.23) | copy-start | bytes 6291460
  953.1 33.5 %copy-start.20 = (bf16[16,256,16,16]{1,3,2,0:T(8,128)(2,1)S(1)}, bf16[16,256,16,16]{1,3,2,0:T(8,128)(2,1)}, u32[]{:S(2)}) copy-start(bf16[16,256,16,16]{1,3,2,0:T(8,128)(2,1)} %get-tuple-element.24) | copy-start | bytes 6291460
  986.5 7.7 copy-start.34
  986.5 7.7 copy-start.36
  986.5 12.2 %copy-start.46 = (f32[768]{0:T(1024)S(1)}, f32[768]{0:T(1024)}, u32[]{:S(2)}) copy-start(f32[768]{0:T(1024)} %get-tuple-element.12) | copy-start | bytes 9220
  986.5 12.2 %copy-start.48 = (f32[256]{0:T(256)S(1)}, f32[256]{0:T(256)}, u32[]{:S(2)}) copy-start(f32[256]{0:T(256)} %get-tuple-element.14) | copy-start | bytes 3076
  1179.6 7.1 copy-start.14
  1179.6 8.7 copy-start.1
Sparse Core Ops, SparseCore 0:
  15.1 104.4 all-gather.2
  121.2 100.5 all-gather.4
  836.9 108.3 reduce-scatter.4
  947.5 108.4 reduce-scatter.2
  1059.0 120.5 all-reduce.3
where the time goes:
time: 1200 us
  matrix products  806 us (67%)
  waiting for transfers between devices  301 us (25%)
  other arithmetic  39.3 us (3%)
  blocking collectives  22.2 us (2%)
  between operations  14.8 us (1%)
    psum x1, waiting for transfers between devices, local_step(): lax.psum((grad_norm_gain, grad_w_dq, grad_q_gain, grad_w_dkv, grad_kv_gai...  116 us
    all_gather x1, waiting for transfers between devices, local_step(): normed_all = lax.all_gather(normed, 'tp', axis=1, tiled=True)  103 us
    dot_general x1, matrix products, heads_backward(): jnp.einsum('bhqk,bkhn->bqhn', grad_scores, k_nope, preferred_element_type...  86.7 us
    dot_general x1, matrix products, heads_backward(): jnp.einsum('bhqk,bqhn->bkhn', grad_scores, q_nope, preferred_element_type...  85.3 us
    dot_general x1, matrix products, heads_backward(): jnp.einsum('bhqk,bkr->bqhr', grad_scores, k_rope, preferred_element_type=...  84 us
    dot_general x1, matrix products, heads_backward(): jnp.einsum('bhqk,bqhr->bkr', grad_scores, q_rope, preferred_element_type=...  83.1 us
    sub x1, matrix products, heads_forward(): attn_prob = jax.nn.softmax(jnp.where(causal, scores, -1e+30), axis=-1)  54.4 us
    all_gather x1, waiting for transfers between devices, local_step(): grad_out_all = lax.all_gather(grad_out, 'tp', axis=1, tiled=True)  45.4 us
  transfers between devices with their start and end apart: 5, of which 4 were waited for; matrix products, arithmetic and copies ran while one was open for 19% of the time, Pallas kernels for 0%

commit v1 on v0

v1 whole, which is shorter than its diff:
```python
import functools

import jax
import jax.numpy as jnp
from jax import lax
from jax.experimental import pallas as pl
from jax.experimental.pallas import tpu as pltpu
from jax.sharding import PartitionSpec as P


NORM_EPS = 1e-6
LOG2_E = 1.4426950408889634
MASKED = -1e30
FORWARD_AHEAD = 4
BACKWARD_AHEAD = 2
F32 = jnp.float32
BF16 = jnp.bfloat16


def norm_forward(value, gain_vec):
    value32 = value.astype(F32)
    inv_rms = lax.rsqrt(jnp.mean(value32 * value32, axis=-1, keepdims=True) + NORM_EPS)
    unit_val = value32 * inv_rms
    return (unit_val * gain_vec.astype(F32)).astype(BF16), unit_val, inv_rms


def norm_backward(grad_norm, unit_val, inv_rms, gain_vec):
    grad_unit = grad_norm * gain_vec.astype(F32)
    grad_in = inv_rms * (grad_unit - unit_val * jnp.mean(grad_unit * unit_val, axis=-1, keepdims=True))
    grad_gain = jnp.sum(grad_norm * unit_val, axis=tuple(range(grad_norm.ndim - 1)))
    return grad_in, grad_gain


def dot(lhs, rhs, lhs_dim, rhs_dim):
    return lax.dot_general(lhs, rhs, (((lhs_dim,), (rhs_dim,)), ((), ())), preferred_element_type=F32)


def whole(early, cross, late, half):
    blank = jnp.zeros((half, half), BF16)
    return jnp.concatenate([jnp.concatenate([early, cross], axis=1), jnp.concatenate([blank, late], axis=1)], axis=0)


def fill_slot(nope, rotary, side):
    blank = jnp.zeros((128 - nope.shape[0] - rotary.shape[0], nope.shape[1]), nope.dtype)
    parts = [nope, rotary, blank] if side == 0 else [rotary, blank, nope]
    return jnp.concatenate(parts, axis=0)


def forward_kernel(dims, score_scale, unroll, lat_ref, wq_ref, wk_ref, wv_ref, wo_ref, cos_ref, sin_ref, q_ref, o_ref, lse_ref, part_ref, k_buf, v_buf):
    q_rank, kv_rank, nope, rope, value = dims
    shards, _, rows, _ = lat_ref.shape
    seq = shards * rows
    half = seq // 2
    head = nope + rope
    mid = rope // 2
    pairs = wk_ref.shape[0] // (2 * nope)
    low = lax.broadcasted_iota(jnp.int32, (seq, 128), 1) < 64
    seen = lax.broadcasted_iota(jnp.int32, (half, half), 0) <= lax.broadcasted_iota(jnp.int32, (half, half), 1)
    key_scale = score_scale * LOG2_E
    q_lat = lat_ref[:, 0, :, :q_rank].reshape(seq, q_rank)
    kv_lat = lat_ref[:, 0, :, q_rank:q_rank + kv_rank].reshape(seq, kv_rank)
    k_rope = lat_ref[:, 0, :, q_rank + kv_rank:].reshape(seq, 128)
    half_q = wq_ref.shape[0] // 2

    def q_step(i, carry):
        at = pl.ds(pl.multiple_of(i * half_q, half_q), half_q)
        q_ref[0, at, :] = dot(wq_ref[at, :], q_lat, 1, 1).astype(BF16)
        return carry

    lax.fori_loop(0, 2, q_step, 0)
    k_buf[...] = dot(kv_lat, wk_ref[...], 1, 1).astype(BF16)
    v_buf[...] = dot(wv_ref[...], kv_lat, 1, 1).astype(BF16)
    cos, sin = cos_ref[...], sin_ref[...]

    def scores(h, side):
        at = h * head
        k_pair = k_buf[:, pl.ds((h - side) * 64, 128)]
        q_nope = q_ref[0, pl.ds(at, nope), :]
        tail = q_ref[0, pl.ds(at + nope, rope), :].astype(F32)
        lead, last = tail[:mid], tail[mid:]
        rotary = jnp.concatenate([lead * cos - last * sin, last * cos + lead * sin], axis=0).astype(BF16)
        q_ref[0, pl.ds(at + nope, rope), :] = rotary
        k = jnp.where(low, k_pair, k_rope) if side == 0 else jnp.where(low, k_rope, k_pair)
        return dot(k, fill_slot(q_nope, rotary, side), 1, 0)

    def attend(h, s):
        early = jnp.where(seen, s[:half, :half], MASKED)
        cross = s[:half, half:]
        late = jnp.where(seen, s[half:, half:], MASKED)
        peak0 = jnp.max(early, axis=0, keepdims=True)
        peak1 = jnp.maximum(jnp.max(cross, axis=0, keepdims=True), jnp.max(late, axis=0, keepdims=True))
        early = jnp.exp2((early - peak0) * key_scale)
        cross = jnp.exp2((cross - peak1) * key_scale)
        late = jnp.exp2((late - peak1) * key_scale)
        total0 = jnp.sum(early, axis=0, keepdims=True)
        total1 = jnp.sum(cross, axis=0, keepdims=True) + jnp.sum(late, axis=0, keepdims=True)
        inv0, inv1 = 1.0 / total0, 1.0 / total1
        prob = whole((early * inv0).astype(BF16), (cross * inv1).astype(BF16), (late * inv1).astype(BF16), half)
        peak = jnp.concatenate([peak0, peak1], axis=1)
        total = jnp.concatenate([total0, total1], axis=1)
        lse_ref[0, pl.ds(h, 1), :] = peak * key_scale + jnp.log2(total)
        return dot(v_buf[pl.ds(h * value, value), :], prob, 1, 0)

    def emit(pair, outs):
        o_pair = jnp.transpose(jnp.concatenate(outs, axis=0)).astype(BF16)
        o_ref[:, 0, :, pl.ds(pair * 128, 128)] = o_pair.reshape(shards, rows, 128)

    def group_step(i, carry):
        first = i * unroll * 2
        count = unroll * 2
        tiles = [scores(first + j, j % 2) if j < FORWARD_AHEAD else None for j in range(count)]
        outs = [None] * count
        for j in range(count):
            if j + FORWARD_AHEAD < count:
                tiles[j + FORWARD_AHEAD] = scores(first + j + FORWARD_AHEAD, (j + FORWARD_AHEAD) % 2)
            outs[j] = attend(first + j, tiles[j])
            if j % 2 == 1:
                emit(i * unroll + j // 2, outs[j - 1:j + 1])
        return carry

    if unroll == pairs:
        group_step(0, 0)
    else:
        lax.fori_loop(0, pairs // unroll, group_step, 0)
    o_all = o_ref[:, 0].reshape(seq, pairs * 2 * value)
    step = 512

    def out_step(i, carry):
        cols = pl.ds(pl.multiple_of(i * step, step), step)
        part_ref[:, 0, :, cols] = dot(o_all, wo_ref[:, cols], 1, 0).astype(BF16).reshape(shards, rows, step)
        return carry

    lax.fori_loop(0, part_ref.shape[3] // step, out_step, 0)


def backward_kernel(dims, score_scale, unroll, lat_ref, dy_ref, q_ref, lse_ref, wq_ref, wk_ref, wv_ref, wo_ref, cos_ref, sin_ref, glat_ref, gwq_ref, gwk_ref, gwv_ref, do_buf, dq_buf, dk_buf, dv_buf, rope_acc, k_buf, kt_buf, v_buf):
    q_rank, kv_rank, nope, rope, value = dims
    shards, _, rows, _ = lat_ref.shape
    seq = shards * rows
    half = seq // 2
    head = nope + rope
    mid = rope // 2
    pairs = wk_ref.shape[0] // (2 * nope)
    low = lax.broadcasted_iota(jnp.int32, (seq, 128), 1) < 64
    seen = lax.broadcasted_iota(jnp.int32, (half, half), 0) <= lax.broadcasted_iota(jnp.int32, (half, half), 1)
    key_scale = score_scale * LOG2_E
    q_lat = lat_ref[:, 0, :, :q_rank].reshape(seq, q_rank)
    kv_lat = lat_ref[:, 0, :, q_rank:q_rank + kv_rank].reshape(seq, kv_rank)
    k_rope = lat_ref[:, 0, :, q_rank + kv_rank:].reshape(seq, 128)
    k_rope_t = jnp.transpose(k_rope.astype(F32))[:rope].astype(BF16)
    dy = dy_ref[:, 0].reshape(seq, dy_ref.shape[3])
    step = 256

    def grad_out_step(i, carry):
        at = pl.ds(pl.multiple_of(i * step, step), step)
        do_buf[at, :] = dot(wo_ref[at, :], dy, 1, 1).astype(BF16)
        return carry

    lax.fori_loop(0, do_buf.shape[0] // step, grad_out_step, 0)
    k_buf[...] = dot(kv_lat, wk_ref[...], 1, 1).astype(BF16)
    kt_buf[...] = dot(wk_ref[...], kv_lat, 1, 1).astype(BF16)
    v_buf[...] = dot(kv_lat, wv_ref[...], 1, 1).astype(BF16)
    rope_acc[...] = jnp.zeros_like(rope_acc)
    cos, sin = cos_ref[...], sin_ref[...]
    none = jnp.zeros((value, seq), BF16)

    def scores(h, side):
        lanes = pl.ds((h - side) * 64, 128)
        q = q_ref[0, pl.ds(h * head, head), :]
        k_pair = k_buf[:, lanes]
        k = jnp.where(low, k_pair, k_rope) if side == 0 else jnp.where(low, k_rope, k_pair)
        do = do_buf[pl.ds(h * value, value), :]
        do_slot = jnp.concatenate([do, none] if side == 0 else [none, do], axis=0)
        s = dot(k, fill_slot(q[:nope], q[nope:], side), 1, 0)
        return s, dot(v_buf[:, lanes], do_slot, 1, 0)

    def finish(h, tiles):
        s, dp = tiles
        lse = lse_ref[0, pl.ds(h, 1), :]
        p_early = jnp.exp2(jnp.where(seen, s[:half, :half], MASKED) * key_scale - lse[:, :half])
        p_cross = jnp.exp2(s[:half, half:] * key_scale - lse[:, half:])
        p_late = jnp.exp2(jnp.where(seen, s[half:, half:], MASKED) * key_scale - lse[:, half:])
        prob = whole(p_early.astype(BF16), p_cross.astype(BF16), p_late.astype(BF16), half)
        dp_early, dp_cross, dp_late = dp[:half, :half], dp[:half, half:], dp[half:, half:]
        sum0 = jnp.sum(p_early * dp_early, axis=0, keepdims=True)
        sum1 = jnp.sum(p_cross * dp_cross, axis=0, keepdims=True) + jnp.sum(p_late * dp_late, axis=0, keepdims=True)
        ds_early = (p_early * (dp_early - sum0) * score_scale).astype(BF16)
        ds_cross = (p_cross * (dp_cross - sum1) * score_scale).astype(BF16)
        ds_late = (p_late * (dp_late - sum1) * score_scale).astype(BF16)
        return prob, whole(ds_early, ds_cross, ds_late, half)

    def products(h, prob, ds):
        rows64 = pl.ds(h * 64, 64)
        grad_v = dot(do_buf[rows64, :], prob, 1, 1)
        dv_buf[rows64, :] = grad_v.astype(BF16)
        grad_k = dot(q_ref[0, pl.ds(h * head, head), :], ds, 1, 1)
        k_t = jnp.concatenate([kt_buf[rows64, :], k_rope_t], axis=0)
        grad_q = dot(k_t, ds, 1, 0)
        lead, last = grad_q[nope:nope + mid], grad_q[nope + mid:]
        dq_buf[pl.ds(h * head, head), :] = jnp.concatenate([grad_q[:nope], lead * cos + last * sin, last * cos - lead * sin], axis=0).astype(BF16)
        dk_buf[rows64, :] = grad_k[:nope].astype(BF16)
        rope_acc[...] += grad_k[nope:]

    def group_step(i, carry):
        count = unroll * 2
        first = i * count
        tiles = [scores(first + j, j % 2) if j < BACKWARD_AHEAD else None for j in range(count)]
        held = None
        for j in range(count):
            if j + BACKWARD_AHEAD < count:
                tiles[j + BACKWARD_AHEAD] = scores(first + j + BACKWARD_AHEAD, (j + BACKWARD_AHEAD) % 2)
            done = finish(first + j, tiles[j])
            if held is not None:
                products(first + j - 1, *held)
            held = done
        products(first + count - 1, *held)
        return carry

    if unroll == pairs:
        group_step(0, 0)
    else:
        lax.fori_loop(0, pairs // unroll, group_step, 0)
    dq, dk, dv = dq_buf[...], dk_buf[...], dv_buf[...]
    glat_ref[:, 0, :, :q_rank] = dot(dq, wq_ref[...], 0, 0).astype(BF16).reshape(shards, rows, q_rank)
    grad_kv = dot(dk, wk_ref[...], 0, 0) + dot(dv, wv_ref[...], 0, 0)
    glat_ref[:, 0, :, q_rank:q_rank + kv_rank] = grad_kv.astype(BF16).reshape(shards, rows, kv_rank)
    padded = jnp.concatenate([rope_acc[...], jnp.zeros((128 - rope, seq), F32)], axis=0)
    glat_ref[:, 0, :, q_rank + kv_rank:] = jnp.transpose(padded).astype(BF16).reshape(shards, rows, 128)

    @pl.when(pl.program_id(0) == 0)
    def _():
        gwq_ref[...] = jnp.zeros_like(gwq_ref)
        gwk_ref[...] = jnp.zeros_like(gwk_ref)
        gwv_ref[...] = jnp.zeros_like(gwv_ref)

    def weight_step(i, carry):
        at = pl.ds(pl.multiple_of(i * step, step), step)
        gwq_ref[at, :] += dot(dq_buf[at, :], q_lat, 1, 0)
        return carry

    lax.fori_loop(0, dq_buf.shape[0] // step, weight_step, 0)
    gwk_ref[...] += dot(dk, kv_lat, 1, 0)
    gwv_ref[...] += dot(dv, kv_lat, 1, 0)


def solution(mesh):
    act_spec = P('dp', 'tp', None)
    head_spec = P(None, 'tp', None)
    in_specs = (act_spec, P(None), P(None, None), P(None), P(None, None), P(None), head_spec, head_spec, head_spec, head_spec, P('tp', None, None), P(None, None), P(None, None), act_spec)
    grad_head_spec = P('dp', 'tp', None)
    out_specs = (act_spec, act_spec, P('dp'), P('dp', None), P('dp'), P('dp', None), P('dp'), grad_head_spec, grad_head_spec, grad_head_spec, grad_head_spec, P(('dp', 'tp'), None, None))

    def local_step(hidden, norm_gain, w_dq, q_gain, w_dkv, kv_gain, w_uq, w_qr, w_uk, w_uv, w_out, rope_cos, rope_sin, grad_out):
        shards = mesh.shape['tp']
        batch, rows, dim = hidden.shape
        q_rank, kv_rank = q_gain.shape[0], kv_gain.shape[0]
        heads, nope = w_uq.shape[1:]
        rope = w_qr.shape[2]
        mid = rope // 2
        value = w_uv.shape[2]
        seq = shards * rows
        tokens = batch * seq
        here = batch * rows
        lat_width = q_rank + kv_rank + 128
        kv_width = kv_rank + rope
        score_scale = (nope + rope) ** -0.5

        x2 = hidden.reshape(here, dim)
        normed, x_unit, x_inv = norm_forward(x2, norm_gain)
        q_latent = dot(normed, w_dq, 1, 0).astype(BF16)
        kv_latent = dot(normed, w_dkv, 1, 0).astype(BF16)
        q_normed, q_unit, q_inv = norm_forward(q_latent, q_gain)
        kv_normed, kv_unit, kv_inv = norm_forward(kv_latent[:, :kv_rank], kv_gain)
        place = lax.axis_index('tp') * rows
        cos_here = jnp.tile(lax.dynamic_slice_in_dim(rope_cos, place, rows, 0), (batch, 1))
        sin_here = jnp.tile(lax.dynamic_slice_in_dim(rope_sin, place, rows, 0), (batch, 1))
        k_in = kv_latent[:, kv_rank:].astype(F32)
        k_lead, k_tail = k_in[:, :mid], k_in[:, mid:]
        k_rot = jnp.concatenate([k_lead * cos_here - k_tail * sin_here, k_tail * cos_here + k_lead * sin_here], axis=1).astype(BF16)
        k_none = jnp.zeros((here, 64 - rope), BF16)
        lat_here = jnp.concatenate([q_normed, kv_normed, k_rot, k_none, k_rot, k_none], axis=1).reshape(batch, rows, lat_width)
        lat_all = lax.all_gather(lat_here, 'tp', axis=0)
        dy_all = lax.all_gather(grad_out, 'tp', axis=0)

        wq = jnp.concatenate([w_uq.transpose(1, 2, 0), w_qr.transpose(1, 2, 0)], axis=1).reshape(heads * (nope + rope), q_rank)
        wk = w_uk.transpose(1, 2, 0).reshape(heads * nope, kv_rank)
        wv = w_uv.transpose(1, 2, 0).reshape(heads * value, kv_rank)
        w_o = w_out.reshape(heads * value, dim)
        weights = (wq, wk, wv, w_o, rope_cos.T, rope_sin.T)
        dims = (q_rank, kv_rank, nope, rope, value)

        def tok(width):
            return pl.BlockSpec((shards, 1, rows, width), lambda b: (0, b, 0, 0))

        def fixed(shape):
            return pl.BlockSpec(shape, lambda b: (0,) * len(shape))

        def per_batch(shape):
            return pl.BlockSpec((1,) + shape, lambda b: (b,) + (0,) * len(shape))

        def out(width):
            return jax.ShapeDtypeStruct((shards, batch, rows, width), BF16)

        weight_specs = [fixed(w.shape) for w in weights]
        attn_flops = 2 * batch * heads * seq * seq * 256
        up_flops = 2 * tokens * heads * ((nope + rope) * q_rank + (nope + value) * kv_rank)
        out_flops = 2 * tokens * heads * value * dim
        q_all, o_all, lse_all, attn_part = pl.pallas_call(
            functools.partial(forward_kernel, dims, score_scale, heads // 2),
            grid=(batch,),
            in_specs=[tok(lat_width)] + weight_specs,
            out_specs=[per_batch((wq.shape[0], seq)), tok(heads * value), per_batch((heads, seq)), tok(dim)],
            out_shape=[jax.ShapeDtypeStruct((batch, wq.shape[0], seq), BF16), out(heads * value), jax.ShapeDtypeStruct((batch, heads, seq), F32), out(dim)],
            scratch_shapes=[pltpu.VMEM((seq, heads * nope), BF16), pltpu.VMEM((heads * value, seq), BF16)],
            compiler_params=pltpu.CompilerParams(dimension_semantics=("arbitrary",)),
            cost_estimate=pl.CostEstimate(flops=attn_flops + up_flops + out_flops, bytes_accessed=70_000_000, transcendentals=batch * heads * seq * seq),
            name="attn_forward",
        )(lat_all, *weights)
        attn_out = lax.psum_scatter(attn_part, 'tp', scatter_dimension=0, tiled=False)
        out_hidden = (hidden.astype(F32) + attn_out.astype(F32)).astype(BF16)

        glat, gwq, gwk, gwv = pl.pallas_call(
            functools.partial(backward_kernel, dims, score_scale, heads // 2),
            grid=(batch,),
            in_specs=[tok(lat_width), tok(dim), per_batch((wq.shape[0], seq)), per_batch((heads, seq))] + weight_specs,
            out_specs=[tok(lat_width), fixed(wq.shape), fixed(wk.shape), fixed(wv.shape)],
            out_shape=[out(lat_width)] + [jax.ShapeDtypeStruct(w.shape, F32) for w in (wq, wk, wv)],
            scratch_shapes=[pltpu.VMEM((heads * value, seq), BF16), pltpu.VMEM((wq.shape[0], seq), BF16), pltpu.VMEM((heads * nope, seq), BF16), pltpu.VMEM((heads * value, seq), BF16), pltpu.VMEM((rope, seq), F32), pltpu.VMEM((seq, heads * nope), BF16), pltpu.VMEM((heads * nope, seq), BF16), pltpu.VMEM((seq, heads * value), BF16)],
            compiler_params=pltpu.CompilerParams(dimension_semantics=("arbitrary",)),
            cost_estimate=pl.CostEstimate(flops=3 * attn_flops + 3 * up_flops + out_flops, bytes_accessed=60_000_000, transcendentals=batch * heads * seq * seq),
            name="attn_backward",
        )(lat_all, dy_all, q_all, lse_all, *weights)
        grad_lat = lax.psum_scatter(glat, 'tp', scatter_dimension=0, tiled=False).reshape(here, lat_width).astype(F32)

        grad_wq = gwq.reshape(heads, nope + rope, q_rank)
        grad_w_uq = grad_wq[:, :nope].transpose(2, 0, 1)
        grad_w_qr = grad_wq[:, nope:].transpose(2, 0, 1)
        grad_w_uk = gwk.reshape(heads, nope, kv_rank).transpose(2, 0, 1)
        grad_w_uv = gwv.reshape(heads, value, kv_rank).transpose(2, 0, 1)
        grad_w_out = dot(o_all.reshape(tokens, heads * value), dy_all.reshape(tokens, dim), 0, 0).reshape(heads, value, dim)

        grad_q_lat, grad_q_gain = norm_backward(grad_lat[:, :q_rank], q_unit, q_inv, q_gain)
        grad_kv_lat, grad_kv_gain = norm_backward(grad_lat[:, q_rank:q_rank + kv_rank], kv_unit, kv_inv, kv_gain)
        gk = grad_lat[:, q_rank + kv_rank:q_rank + kv_rank + rope]
        gk_lead, gk_tail = gk[:, :mid], gk[:, mid:]
        grad_q_lat = grad_q_lat.astype(BF16)
        grad_kv_all = jnp.concatenate([grad_kv_lat, gk_lead * cos_here + gk_tail * sin_here, gk_tail * cos_here - gk_lead * sin_here], axis=1).astype(BF16)
        own = dim // shards
        own_kv = kv_width // shards * dim // q_rank
        part_dq = dot(normed, grad_q_lat, 0, 0).astype(BF16).reshape(shards, own, q_rank)
        part_dkv = dot(grad_kv_all, normed, 0, 0).astype(BF16).reshape(shards, own_kv, q_rank)
        down_sum = lax.psum_scatter(jnp.concatenate([part_dq, part_dkv], axis=1), 'tp', scatter_dimension=0, tiled=False)
        grad_normed = dot(grad_q_lat, w_dq, 1, 1) + dot(grad_kv_all, w_dkv, 1, 1)
        grad_x_norm, grad_norm_gain = norm_backward(grad_normed, x_unit, x_inv, norm_gain)
        grad_hidden = grad_out.reshape(here, dim).astype(F32) + grad_x_norm

        gains = jnp.concatenate([grad_norm_gain, grad_q_gain, grad_kv_gain])
        gain_rows = -(-gains.shape[0] // q_rank)
        gains = jnp.pad(gains, (0, gain_rows * q_rank - gains.shape[0])).reshape(gain_rows, q_rank)
        high = lax.reduce_precision(gains, 8, 7)
        middle = lax.reduce_precision(gains - high, 8, 7)
        tail = gains - high - middle
        packed = jnp.concatenate([down_sum, high.astype(BF16), middle.astype(BF16), tail.astype(BF16)], axis=0)
        gathered = lax.all_gather(packed, 'tp', axis=0)
        grad_w_dq = gathered[:, :own].reshape(dim, q_rank).astype(F32)
        grad_w_dkv = gathered[:, own:own + own_kv].reshape(kv_width, dim).astype(F32).T
        terms = gathered[:, own + own_kv:].astype(F32).reshape(shards, 3, gain_rows * q_rank)
        sums = jnp.sum(terms[:, 0] + terms[:, 1] + terms[:, 2], axis=0)
        g_norm = sums[:dim]
        g_q = sums[dim:dim + q_rank]
        g_kv = sums[dim + q_rank:dim + q_rank + kv_rank]
        return (out_hidden, grad_hidden.reshape(batch, rows, dim), g_norm, grad_w_dq, g_q, grad_w_dkv, g_kv, grad_w_uq, grad_w_qr, grad_w_uk, grad_w_uv, grad_w_out)

    return jax.shard_map(local_step, mesh=mesh, in_specs=in_specs, out_specs=out_specs, check_vma=False)
```

time: 1200 us -> 599 us (0.50)
  matrix products: 806 us -> 44.9 us
  Pallas kernels: 0 us -> 226 us
  waiting for transfers between devices: 301 us -> 238 us
  local copies, waits for them, and re-layouts: 11.7 us -> 37.2 us
  blocking collectives: 22.2 us -> 0 us
    dot_general x29 -> x7, matrix products: 752 us -> 44.9 us  [dot(): lax.dot_general(lhs, rhs, (((lhs_dim,), (rhs_dim,)), ((), ())), preferred...]
    pallas_call x0 -> x2, Pallas kernels: none -> 226 us  [the longest x1 138 us: local_step(): pl.pallas_call(functools.partial(backward_kernel, dims, score_scale, head...]
    psum x1 -> x0, waiting for transfers between devices: 116 us -> none  [local_step(): lax.psum((grad_norm_gain, grad_w_dq, grad_q_gain, grad_w_dkv, grad_kv_gai...]
    reduce_scatter x2 -> x3, waiting for transfers between devices: 35.1 us -> 139 us  [the longest x1 59.8 us: local_step(): lax.psum_scatter(attn_part, 'tp', scatter_dimension=0, tiled=False)]
    sub x1 -> x0, matrix products: 54.4 us -> none  [heads_forward(): attn_prob = jax.nn.softmax(jnp.where(causal, scores, -1e+30), axis=-1)]
    all_gather x2 -> x3, waiting for transfers between devices: 148 us -> 98 us  [the longest x1 51.6 us: local_step(): lat_all = lax.all_gather(lat_here, 'tp', axis=0)]
    psum x1 -> x0, blocking collectives: 22.2 us -> none  [local_step(): lax.psum((grad_norm_gain, grad_w_dq, grad_q_gain, grad_w_dkv, grad_kv_gai...]
    dot_general x0 -> x1, local copies, waits for them, and re-layouts: none -> 12 us  [dot(): lax.dot_general(lhs, rhs, (((lhs_dim,), (rhs_dim,)), ((), ())), preferred...]
  transfers between devices with their start and end apart: 5 -> 6, of which waited for: 4 -> 6; matrix products, arithmetic and copies ran while one was open for 19% -> 12% of each run, Pallas kernels for 0% -> 15%
where the time goes in v1:
time: 599 us; the launch traced here: 598 us
  waiting for transfers between devices  238 us (40%)
  Pallas kernels  226 us (38%)
  matrix products  44.9 us (7%)
  local copies, waits for them, and re-layouts  37.2 us (6%)
  other arithmetic  36.1 us (6%)
  between operations  14.5 us (2%)
    pallas_call x1, Pallas kernels, local_step(): pl.pallas_call(functools.partial(backward_kernel, dims, score_scale, head...  138 us
    pallas_call x1, Pallas kernels, local_step(): pl.pallas_call(functools.partial(forward_kernel, dims, score_scale, heads...  87.5 us
    reduce_scatter x1, waiting for transfers between devices, local_step(): lax.psum_scatter(attn_part, 'tp', scatter_dimension=0, tiled=False)  59.8 us
    reduce_scatter x1, waiting for transfers between devices, local_step(): lax.psum_scatter(glat, 'tp', scatter_dimension=0, tiled=False)  54.1 us
    all_gather x1, waiting for transfers between devices, local_step(): lat_all = lax.all_gather(lat_here, 'tp', axis=0)  51.6 us
    dot_general x7, matrix products, dot(): lax.dot_general(lhs, rhs, (((lhs_dim,), (rhs_dim,)), ((), ())), preferred...  44.9 us
    all_gather x1, waiting for transfers between devices, local_step(): gathered = lax.all_gather(packed, 'tp', axis=0)  32.6 us
    reduce_scatter x1, waiting for transfers between devices, local_step(): lax.psum_scatter(jnp.concatenate([part_dq, part_dkv], axis=1), 'tp', scat...  25 us
  transfers between devices with their start and end apart: 6, of which 6 were waited for; matrix products, arithmetic and copies ran while one was open for 12% of the time, Pallas kernels for 15%

profile of v1, /device:TPU:81, one launch (start us, length us, event | category | flops | bytes accessed | tf_op | source)
XLA Modules:
  0.0 597.7 jit_solution(1201531708273831083)
XLA Ops:
  7.3 0.8 convert_element_type.103
  8.1 2.3 multiply_reduce_fusion.2
  10.4 0.1 rsqrt.28
  10.5 0.6 copy-done.14
  11.1 2.4 multiply_convert_fusion
  13.5 1.5 convolution_convert_fusion.3
  15.1 0.1 fusion.22
  15.2 0.7 slice_convert_fusion.2
  15.9 0.7 copy-done.19
  16.7 2.3 fusion.11
  19.0 0.1 constant_dynamic-slice_fusion
  19.1 0.1 copy.36
  19.2 0.1 copy.35
  19.3 0.8 fusion.16
  20.1 0.2 fusion.5
  20.4 1.9 fusion.26
  22.2 0.7 broadcast_in_dim.2
  22.9 3.1 concatenate.22
  26.1 0.7 all-gather.9.cloned.1.call-update
  26.9 0.2 reduce-scatter.6.cloned.1.call-start
  27.1 3.0 pad_maximum_fusion.1
  30.1 51.6 %all-gather.7.cloned.1.call-done.lat_ref = bf16[8,16,32,1152]{3,2,1,0:T(8,128)(2,1)} async-done(((bf16[1,16,32,1152]{3,2,1,0:T(8,128)(2,1)}), bf16[8,16,32,1152]{3,2,1,0:T(8,128)(2,1)}) %all-gather.7.cloned.1.call-update) | async-done | bytes 9437200 | tf_op jit(solution)/shard_map/all_gather | solution.py:282
  81.7 87.5 %attn_forward.1 = (bf16[16,1536,256]{2,1,0:T(8,128)(2,1)}, bf16[8,16,32,1024]{3,2,1,0:T(8,128)(2,1)}, f32[16,16,256]{2,1,0:T(8,128)}, bf16[8,16,32,2560]{3,2,1,0:T(8,128)(2,1)}) custom-call(bf16[8,16,32,1152]{3,2,1,0:T(8,128)(2,1)} %all-gather.7.cloned.1.call-done.lat_ref, bf16[1536,768]{1,0:T(8,128)(2,1)} %bitcast.115, bf16[1024,256]{1,0:T(8,128)(2,1)} %bitcast.129, ...), custom_call_target="tpu_custom_call" | custom-call | flops 44023414784 | bytes 70000000 | tf_op jit(solution)/shard_map/attn_forward/pallas_call | solution.py:308
  169.3 13.7 %all-gather.9.cloned.1.call-done = bf16[128,32,2560]{2,1,0:T(8,128)(2,1)} async-done(((bf16[16,32,2560]{2,1,0:T(8,128)(2,1)}), bf16[128,32,2560]{2,1,0:T(8,128)(2,1)}) %all-gather.9.cloned.1.call-update) | async-done | bytes 20971536 | tf_op jit(solution)/shard_map/all_gather | solution.py:283
  183.0 138.1 %attn_backward.1 = (bf16[8,16,32,1152]{3,2,1,0:T(8,128)(2,1)}, f32[1536,768]{1,0:T(8,128)}, f32[1024,256]{1,0:T(8,128)}, f32[1024,256]{1,0:T(8,128)}) custom-call(bf16[8,16,32,1152]{3,2,1,0:T(8,128)(2,1)} %all-gather.7.cloned.1.call-done.lat_ref, bf16[8,16,32,2560]{3,2,1,0:T(8,128)(2,1)} %bitcast.125, bf16[16,1536,256]{2,1,0:T(8,128)(2,1)} %get-tuple-element.21.q_ref, ...), custom_call_target="tpu_custom_call" | custom-call | flops 89120571392 | bytes 60000000 | tf_op jit(solution)/shard_map/attn_backward/pallas_call | solution.py:322
  321.2 0.3 reduce-scatter.8.cloned.1.call-start
  321.5 54.1 %reduce-scatter.6.cloned.1.call-done = bf16[1,16,32,1152]{3,2,1,0:T(8,128)(2,1)} async-done(((bf16[8,16,32,1152]{3,2,1,0:T(8,128)(2,1)}), bf16[1,16,32,1152]{3,2,1,0:T(8,128)(2,1)}) %reduce-scatter.6.cloned.1.call-update) | async-done | bytes 1179664 | tf_op jit(solution)/shard_map/reduce_scatter | solution.py:333
  375.5 1.4 convert.28
  377.0 0.6 fusion.10
  377.6 0.2 fusion.28
  377.7 0.3 fusion.21
  378.0 0.3 copy-done.3
  378.4 0.2 fusion.20
  378.6 1.0 copy-done.5
  379.6 1.0 convolution_convert_fusion.1
  380.6 2.6 reshape.151
  383.2 5.0 convolution_convert_fusion
  388.1 2.8 pad_maximum_fusion
  391.0 0.1 reduce-scatter.4.cloned.1.call-start
  391.0 0.6 reduce-scatter.4.cloned.1.call-update
  391.6 0.3 all-gather.11.cloned.1.call-start
  392.0 0.2 copy-done.10
  392.2 5.1 fusion.36
  397.3 3.8 multiply_reduce_fusion
  401.1 25.0 %reduce-scatter.8.cloned.1.call-done = bf16[1,440,768]{2,1,0:T(8,128)(2,1)} async-done(((bf16[8,440,768]{2,1,0:T(8,128)(2,1)}), bf16[1,440,768]{2,1,0:T(8,128)(2,1)}) %reduce-scatter.8.cloned.1.call-update) | async-done | bytes 675856 | tf_op jit(solution)/shard_map/reduce_scatter | solution.py:352
  426.0 2.0 maximum_bitcast_fusion
  428.1 12.0 %copy.37 = bf16[1024,4096]{1,0:T(8,128)(2,1)} copy(bf16[1024,4096]{0,1:T(8,128)(2,1)} %bitcast.107) | data formatting | bytes 16777216 | tf_op jit(solution)/shard_map/dot_general | solution.py:35
  440.1 2.9 slice_bitcast_fusion.1
  443.0 4.7 slice_bitcast_fusion
  447.7 26.3 %fusion.38 = f32[16,64,2560]{2,1,0:T(8,128)} fusion(bf16[16,64,4096]{2,1,0:T(8,128)(2,1)S(1)} %bitcast.108, bf16[4096,2560,1]{1,0,2:T(8,128)(2,1)} %bitcast.126), kind=kOutput, calls=%fused_computation.89 | convolution fusion | flops 21474836480 | bytes 39845888 | tf_op jit(solution)/shard_map/dot_general | solution.py:35
  474.0 4.4 convert_add_fusion
  478.4 59.8 %reduce-scatter.4.cloned.1.call-done = bf16[1,16,32,2560]{3,2,1,0:T(8,128)(2,1)} async-done(((bf16[8,16,32,2560]{3,2,1,0:T(8,128)(2,1)}), bf16[1,16,32,2560]{3,2,1,0:T(8,128)(2,1)}) %reduce-scatter.4.cloned.1.call-update) | async-done | bytes 2621456 | tf_op jit(solution)/shard_map/reduce_scatter | solution.py:319
  538.2 4.8 fusion
  543.0 32.6 %all-gather.11.cloned.1.call-done = bf16[8,455,768]{2,1,0:T(8,128)(2,1)} async-done(((bf16[1,455,768]{2,1,0:T(8,128)(2,1)}), bf16[8,455,768]{2,1,0:T(8,128)(2,1)}) %all-gather.11.cloned.1.call-update) | async-done | bytes 5591056 | tf_op jit(solution)/shard_map/all_gather | solution.py:364
  575.6 1.0 slice_convert_fusion.1
  576.6 0.2 reshape.165
  576.8 0.3 fusion.31
  577.1 0.6 slice.91
  577.7 0.6 slice.93
  578.3 0.6 slice.95
  578.9 2.1 slice-done.4
  581.0 4.1 bitcast_convert_fusion
  585.1 1.8 slice_convert_fusion
  586.9 4.0 reshape.167
  (65 shorter events, 0.5 us)
Async XLA Ops:
  7.2 6.3 %copy-start = (bf16[2560,288]{0,1:T(8,128)(2,1)S(1)}, bf16[2560,288]{0,1:T(8,128)(2,1)}, u32[]{:S(2)}) copy-start(bf16[2560,288]{0,1:T(8,128)(2,1)} %param.18) | copy-start | bytes 4423684
  7.2 74.5 %all-gather.7.cloned.1.call-start = ((), (), s32[]{:S(2)}) async-start(), calls=%async_computation.3 | async-start | bytes 10616832 | tf_op jit(solution)/shard_map/all_gather | solution.py:282
  8.1 2.4 copy-start.12
  10.5 0.6 copy-start.14
  13.5 2.4 copy-start.4
  13.5 3.2 copy-start.19
  16.7 2.3 copy-start.18
  16.7 2.3 copy-start.20
  16.7 2.4 copy-start.16
  16.7 2.4 copy-start.17
  19.0 358.0 %copy-start.9 = (bf16[512,768]{1,0:T(8,128)(2,1)}, bf16[512,768]{1,0:T(8,128)(2,1)S(1)}, u32[]{:S(2)}) copy-start(bf16[512,768]{1,0:T(8,128)(2,1)S(1)} %get-tuple-element.42) | copy-start | bytes 2359300
  26.0 1.1 copy-start.11
  26.1 156.9 %all-gather.9.cloned.1.call-start = ((), (), s32[]{:S(2)}) async-start(), calls=%async_computation.7 | async-start | bytes 23592960 | tf_op jit(solution)/shard_map/all_gather | solution.py:283
  26.9 348.7 %reduce-scatter.6.cloned.1.call-start = ((), (), s32[]{:S(2)}) async-start(), calls=%async_computation.5 | async-start | bytes 10616832 | tf_op jit(solution)/shard_map/reduce_scatter | solution.py:333
  321.2 104.9 %reduce-scatter.8.cloned.1.call-start = ((), (), s32[]{:S(2)}) async-start(), calls=%async_computation.6 | async-start | bytes 6082560 | tf_op jit(solution)/shard_map/reduce_scatter | solution.py:352
  377.0 1.4 copy-start.3
  377.0 2.6 copy-start.5
  383.2 5.0 copy-start.8
  391.0 147.2 %reduce-scatter.4.cloned.1.call-start = ((), (), s32[]{:S(2)}) async-start(), calls=%async_computation.4 | async-start | bytes 23592960 | tf_op jit(solution)/shard_map/reduce_scatter | solution.py:319
  391.0 1.1 copy-start.10
  391.6 5.6 copy-start.13
  391.6 5.6 copy-start.15
  391.6 184.0 %all-gather.11.cloned.1.call-start = ((), (), s32[]{:S(2)}) async-start(), calls=%async_computation.8 | async-start | bytes 6303744 | tf_op jit(solution)/shard_map/all_gather | solution.py:364
  392.2 5.1 copy-start.1
  440.1 7.6 %copy-start.7 = (bf16[1024,4096]{1,0:T(8,128)(2,1)S(1)}, bf16[1024,4096]{1,0:T(8,128)(2,1)}, u32[]{:S(2)}) copy-start(bf16[1024,4096]{1,0:T(8,128)(2,1)} %copy.37) | copy-start | bytes 25165828
  447.7 26.3 %slice-start = ((s8[5242880]{0:T(1024)(128)(4,1)}), s8[4194304]{0:T(1024)(128)(4,1)S(1)}, s32[]{:S(2)}) async-start(s8[5242880]{0:T(1024)(128)(4,1)} %bitcast.103), calls=%async_computation.9 | async-start | bytes 8388608
  447.7 26.3 %copy-start.2 = (bf16[16,32,2560]{2,1,0:T(8,128)(2,1)S(1)}, bf16[16,32,2560]{2,1,0:T(8,128)(2,1)}, u32[]{:S(2)}) copy-start(bf16[16,32,2560]{2,1,0:T(8,128)(2,1)} %param.14) | copy-start | bytes 7864324
  447.7 26.3 %slice-start.1 = ((s8[5242880]{0:T(1024)(128)(4,1)}), s8[1048576]{0:T(1024)(128)(4,1)S(1)}, s32[]{:S(2)}) async-start(s8[5242880]{0:T(1024)(128)(4,1)} %bitcast.103), calls=%async_computation.10 | async-start | bytes 2097152
  447.7 26.3 %copy-start.6 = (bf16[16,32,2560]{2,1,0:T(8,128)(2,1)S(1)}, bf16[16,32,2560]{2,1,0:T(8,128)(2,1)}, u32[]{:S(2)}) copy-start(bf16[16,32,2560]{2,1,0:T(8,128)(2,1)} %param.27) | copy-start | bytes 7864324
  578.8 2.1 slice-start.4
  578.9 6.2 %slice-start.2 = ((s8[5603328]{0:T(1024)(128)(4,1)}), s8[4194304]{0:T(1024)(128)(4,1)S(1)}, s32[]{:S(2)}) async-start(s8[5603328]{0:T(1024)(128)(4,1)} %bitcast.105), calls=%async_computation.11 | async-start | bytes 8388608
  581.0 4.1 slice-start.3
Sparse Core Ops, SparseCore 0:
  26.2 55.5 all-gather.6
  83.3 99.6 all-gather.8
  321.3 54.1 reduce-scatter.5
  391.1 34.9 reduce-scatter.7
  428.3 109.8 reduce-scatter.3
  540.2 35.3 all-gather.10

commit v2 on v1

--- a/solution.py
+++ b/solution.py
@@ -133,7 +133,7 @@
     lax.fori_loop(0, part_ref.shape[3] // step, out_step, 0)
 
 
-def backward_kernel(dims, score_scale, unroll, lat_ref, dy_ref, q_ref, lse_ref, wq_ref, wk_ref, wv_ref, wo_ref, cos_ref, sin_ref, glat_ref, gwq_ref, gwk_ref, gwv_ref, do_buf, dq_buf, dk_buf, dv_buf, rope_acc, k_buf, kt_buf, v_buf):
+def backward_kernel(dims, score_scale, unroll, lat_ref, dy_ref, q_ref, lse_ref, wq_ref, wk_ref, wv_ref, wo_ref, cos_ref, sin_ref, glat_ref, dq_ref, dk_ref, dv_ref, do_buf, rope_acc, k_buf, kt_buf, v_buf):
     q_rank, kv_rank, nope, rope, value = dims
     shards, _, rows, _ = lat_ref.shape
     seq = shards * rows
@@ -144,7 +144,6 @@
     low = lax.broadcasted_iota(jnp.int32, (seq, 128), 1) < 64
     seen = lax.broadcasted_iota(jnp.int32, (half, half), 0) <= lax.broadcasted_iota(jnp.int32, (half, half), 1)
     key_scale = score_scale * LOG2_E
-    q_lat = lat_ref[:, 0, :, :q_rank].reshape(seq, q_rank)
     kv_lat = lat_ref[:, 0, :, q_rank:q_rank + kv_rank].reshape(seq, kv_rank)
     k_rope = lat_ref[:, 0, :, q_rank + kv_rank:].reshape(seq, 128)
     k_rope_t = jnp.transpose(k_rope.astype(F32))[:rope].astype(BF16)
@@ -192,13 +191,13 @@
     def products(h, prob, ds):
         rows64 = pl.ds(h * 64, 64)
         grad_v = dot(do_buf[rows64, :], prob, 1, 1)
-        dv_buf[rows64, :] = grad_v.astype(BF16)
+        dv_ref[0, rows64, :] = grad_v.astype(BF16)
         grad_k = dot(q_ref[0, pl.ds(h * head, head), :], ds, 1, 1)
         k_t = jnp.concatenate([kt_buf[rows64, :], k_rope_t], axis=0)
         grad_q = dot(k_t, ds, 1, 0)
         lead, last = grad_q[nope:nope + mid], grad_q[nope + mid:]
-        dq_buf[pl.ds(h * head, head), :] = jnp.concatenate([grad_q[:nope], lead * cos + last * sin, last * cos - lead * sin], axis=0).astype(BF16)
-        dk_buf[rows64, :] = grad_k[:nope].astype(BF16)
+        dq_ref[0, pl.ds(h * head, head), :] = jnp.concatenate([grad_q[:nope], lead * cos + last * sin, last * cos - lead * sin], axis=0).astype(BF16)
+        dk_ref[0, rows64, :] = grad_k[:nope].astype(BF16)
         rope_acc[...] += grad_k[nope:]
 
     def group_step(i, carry):
@@ -220,27 +219,66 @@
         group_step(0, 0)
     else:
         lax.fori_loop(0, pairs // unroll, group_step, 0)
-    dq, dk, dv = dq_buf[...], dk_buf[...], dv_buf[...]
+    dq, dk, dv = dq_ref[0], dk_ref[0], dv_ref[0]
     glat_ref[:, 0, :, :q_rank] = dot(dq, wq_ref[...], 0, 0).astype(BF16).reshape(shards, rows, q_rank)
     grad_kv = dot(dk, wk_ref[...], 0, 0) + dot(dv, wv_ref[...], 0, 0)
     glat_ref[:, 0, :, q_rank:q_rank + kv_rank] = grad_kv.astype(BF16).reshape(shards, rows, kv_rank)
     padded = jnp.concatenate([rope_acc[...], jnp.zeros((128 - rope, seq), F32)], axis=0)
     glat_ref[:, 0, :, q_rank + kv_rank:] = jnp.transpose(padded).astype(BF16).reshape(shards, rows, 128)
 
+
+def weights_kernel(q_rank, kv_rank, lat_ref, dq_ref, dk_ref, dv_ref, gwq_ref, gwk_ref, gwv_ref):
+    shards, _, rows, _ = lat_ref.shape
+    seq = shards * rows
+    q_lat = lat_ref[:, 0, :, :q_rank].reshape(seq, q_rank)
+    kv_lat = lat_ref[:, 0, :, q_rank:q_rank + kv_rank].reshape(seq, kv_rank)
+    step = 256
+
     @pl.when(pl.program_id(0) == 0)
     def _():
         gwq_ref[...] = jnp.zeros_like(gwq_ref)
         gwk_ref[...] = jnp.zeros_like(gwk_ref)
         gwv_ref[...] = jnp.zeros_like(gwv_ref)
 
-    def weight_step(i, carry):
+    def q_step(i, carry):
         at = pl.ds(pl.multiple_of(i * step, step), step)
-        gwq_ref[at, :] += dot(dq_buf[at, :], q_lat, 1, 0)
-        return carry
-
-    lax.fori_loop(0, dq_buf.shape[0] // step, weight_step, 0)
-    gwk_ref[...] += dot(dk, kv_lat, 1, 0)
-    gwv_ref[...] += dot(dv, kv_lat, 1, 0)
+        gwq_ref[at, :] += dot(dq_ref[0, at, :], q_lat, 1, 0)
+        return carry
+
+    lax.fori_loop(0, gwq_ref.shape[0] // step, q_step, 0)
+    gwk_ref[...] += dot(dk_ref[0], kv_lat, 1, 0)
+    gwv_ref[...] += dot(dv_ref[0], kv_lat, 1, 0)
+
+
+def latent_kernel(axis, x_ref, gain_ref, wdq_ref, wdkv_ref, qgain_ref, kvgain_ref, tab_ref, normed_ref, qlat_ref, kvlat_ref, lat_ref, wr_buf):
+    batch, rows, dim = x_ref.shape
+    count = batch * rows
+    q_rank, kv_rank = qgain_ref.shape[1], kvgain_ref.shape[1]
+    rope = wdkv_ref.shape[0] - kv_rank
+
+    @pl.when(pl.program_id(0) == 0)
+    def _():
+        wr_buf[...] = jnp.zeros_like(wr_buf)
+        wr_buf[:rope, :] = wdkv_ref[kv_rank:, :]
+
+    def unit(v):
+        return v * lax.rsqrt(jnp.mean(v * v, axis=-1, keepdims=True) + NORM_EPS)
+
+    x = x_ref[...].reshape(count, dim).astype(F32)
+    normed = (unit(x) * gain_ref[...].astype(F32)).astype(BF16)
+    normed_ref[...] = normed
+    q_lat = dot(normed, wdq_ref[...], 1, 0).astype(BF16)
+    kv_lat = dot(normed, wdkv_ref[:kv_rank, :], 1, 1).astype(BF16)
+    k_in = dot(normed, wr_buf[...], 1, 1).astype(BF16).astype(F32)
+    qlat_ref[...] = q_lat
+    kvlat_ref[...] = kv_lat
+    lat_ref[:, :, :q_rank] = (unit(q_lat.astype(F32)) * qgain_ref[...].astype(F32)).astype(BF16).reshape(batch, rows, q_rank)
+    lat_ref[:, :, q_rank:q_rank + kv_rank] = (unit(kv_lat.astype(F32)) * kvgain_ref[...].astype(F32)).astype(BF16).reshape(batch, rows, kv_rank)
+    here = pl.ds(pl.multiple_of(lax.axis_index(axis) * rows, rows), rows)
+    tab = jnp.concatenate([tab_ref[here, :]] * batch, axis=0)
+    mid = rope // 2
+    k_rot = k_in * tab[:, :128] + pltpu.roll(k_in, 128 - mid, 1) * tab[:, 128:256] + pltpu.roll(k_in, mid, 1) * tab[:, 256:]
+    lat_ref[:, :, q_rank + kv_rank:] = (k_rot + pltpu.roll(k_rot, 64, 1)).astype(BF16).reshape(batch, rows, 128)
 
 
 def solution(mesh):
@@ -266,19 +304,21 @@
         score_scale = (nope + rope) ** -0.5
 
         x2 = hidden.reshape(here, dim)
-        normed, x_unit, x_inv = norm_forward(x2, norm_gain)
-        q_latent = dot(normed, w_dq, 1, 0).astype(BF16)
-        kv_latent = dot(normed, w_dkv, 1, 0).astype(BF16)
-        q_normed, q_unit, q_inv = norm_forward(q_latent, q_gain)
-        kv_normed, kv_unit, kv_inv = norm_forward(kv_latent[:, :kv_rank], kv_gain)
-        place = lax.axis_index('tp') * rows
-        cos_here = jnp.tile(lax.dynamic_slice_in_dim(rope_cos, place, rows, 0), (batch, 1))
-        sin_here = jnp.tile(lax.dynamic_slice_in_dim(rope_sin, place, rows, 0), (batch, 1))
-        k_in = kv_latent[:, kv_rank:].astype(F32)
-        k_lead, k_tail = k_in[:, :mid], k_in[:, mid:]
-        k_rot = jnp.concatenate([k_lead * cos_here - k_tail * sin_here, k_tail * cos_here + k_lead * sin_here], axis=1).astype(BF16)
-        k_none = jnp.zeros((here, 64 - rope), BF16)
-        lat_here = jnp.concatenate([q_normed, kv_normed, k_rot, k_none, k_rot, k_none], axis=1).reshape(batch, rows, lat_width)
+        none = jnp.zeros((seq, 128 - rope), F32)
+        half_none = jnp.zeros((seq, mid), F32)
+        key_tab = jnp.concatenate([rope_cos, rope_cos, none, -rope_sin, half_none, none, half_none, rope_sin, none], axis=1)
+        some = min(batch, 4)
+        normed, q_latent, kv_latent, lat_here = pl.pallas_call(
+            functools.partial(latent_kernel, 'tp'),
+            grid=(batch // some,),
+            in_specs=[pl.BlockSpec((some, rows, dim), lambda b: (b, 0, 0))] + [pl.BlockSpec(shape, lambda b: (0, 0)) for shape in ((1, dim), w_dq.shape, (kv_width, dim), (1, q_rank), (1, kv_rank), key_tab.shape)],
+            out_specs=[pl.BlockSpec((some * rows, width), lambda b: (b, 0)) for width in (dim, q_rank, kv_rank)] + [pl.BlockSpec((some, rows, lat_width), lambda b: (b, 0, 0))],
+            out_shape=[jax.ShapeDtypeStruct((here, width), BF16) for width in (dim, q_rank, kv_rank)] + [jax.ShapeDtypeStruct((batch, rows, lat_width), BF16)],
+            scratch_shapes=[pltpu.VMEM((128, dim), BF16)],
+            compiler_params=pltpu.CompilerParams(dimension_semantics=("arbitrary",)),
+            cost_estimate=pl.CostEstimate(flops=2 * here * dim * (q_rank + kv_width), bytes_accessed=12_000_000, transcendentals=here),
+            name="latents",
+        )(hidden, norm_gain[None], w_dq, w_dkv.T, q_gain[None], kv_gain[None], key_tab)
         lat_all = lax.all_gather(lat_here, 'tp', axis=0)
         dy_all = lax.all_gather(grad_out, 'tp', axis=0)
 
@@ -319,19 +359,30 @@
         attn_out = lax.psum_scatter(attn_part, 'tp', scatter_dimension=0, tiled=False)
         out_hidden = (hidden.astype(F32) + attn_out.astype(F32)).astype(BF16)
 
-        glat, gwq, gwk, gwv = pl.pallas_call(
+        glat, dq_all, dk_all, dv_all = pl.pallas_call(
             functools.partial(backward_kernel, dims, score_scale, heads // 2),
             grid=(batch,),
             in_specs=[tok(lat_width), tok(dim), per_batch((wq.shape[0], seq)), per_batch((heads, seq))] + weight_specs,
-            out_specs=[tok(lat_width), fixed(wq.shape), fixed(wk.shape), fixed(wv.shape)],
-            out_shape=[out(lat_width)] + [jax.ShapeDtypeStruct(w.shape, F32) for w in (wq, wk, wv)],
-            scratch_shapes=[pltpu.VMEM((heads * value, seq), BF16), pltpu.VMEM((wq.shape[0], seq), BF16), pltpu.VMEM((heads * nope, seq), BF16), pltpu.VMEM((heads * value, seq), BF16), pltpu.VMEM((rope, seq), F32), pltpu.VMEM((seq, heads * nope), BF16), pltpu.VMEM((heads * nope, seq), BF16), pltpu.VMEM((seq, heads * value), BF16)],
+            out_specs=[tok(lat_width)] + [per_batch((w.shape[0], seq)) for w in (wq, wk, wv)],
+            out_shape=[out(lat_width)] + [jax.ShapeDtypeStruct((batch, w.shape[0], seq), BF16) for w in (wq, wk, wv)],
+            scratch_shapes=[pltpu.VMEM((heads * value, seq), BF16), pltpu.VMEM((rope, seq), F32), pltpu.VMEM((seq, heads * nope), BF16), pltpu.VMEM((heads * nope, seq), BF16), pltpu.VMEM((seq, heads * value), BF16)],
             compiler_params=pltpu.CompilerParams(dimension_semantics=("arbitrary",)),
-            cost_estimate=pl.CostEstimate(flops=3 * attn_flops + 3 * up_flops + out_flops, bytes_accessed=60_000_000, transcendentals=batch * heads * seq * seq),
+            cost_estimate=pl.CostEstimate(flops=3 * attn_flops + 2 * up_flops + out_flops, bytes_accessed=60_000_000, transcendentals=batch * heads * seq * seq),
             name="attn_backward",
         )(lat_all, dy_all, q_all, lse_all, *weights)
-        grad_lat = lax.psum_scatter(glat, 'tp', scatter_dimension=0, tiled=False).reshape(here, lat_width).astype(F32)
-
+        grad_lat = lax.psum_scatter(glat, 'tp', scatter_dimension=0, tiled=False)
+        grad_lat = grad_lat.reshape(here, lat_width).astype(F32)
+
+        gwq, gwk, gwv = pl.pallas_call(
+            functools.partial(weights_kernel, q_rank, kv_rank),
+            grid=(batch,),
+            in_specs=[tok(lat_width)] + [per_batch((w.shape[0], seq)) for w in (wq, wk, wv)],
+            out_specs=[fixed(w.shape) for w in (wq, wk, wv)],
+            out_shape=[jax.ShapeDtypeStruct(w.shape, F32) for w in (wq, wk, wv)],
+            compiler_params=pltpu.CompilerParams(dimension_semantics=("arbitrary",)),
+            cost_estimate=pl.CostEstimate(flops=up_flops, bytes_accessed=50_000_000, transcendentals=0),
+            name="head_weight_grads",
+        )(lat_all, dq_all, dk_all, dv_all)
         grad_wq = gwq.reshape(heads, nope + rope, q_rank)
         grad_w_uq = grad_wq[:, :nope].transpose(2, 0, 1)
         grad_w_qr = grad_wq[:, nope:].transpose(2, 0, 1)
@@ -339,6 +390,12 @@
         grad_w_uv = gwv.reshape(heads, value, kv_rank).transpose(2, 0, 1)
         grad_w_out = dot(o_all.reshape(tokens, heads * value), dy_all.reshape(tokens, dim), 0, 0).reshape(heads, value, dim)
 
+        _, x_unit, x_inv = norm_forward(x2, norm_gain)
+        _, q_unit, q_inv = norm_forward(q_latent, q_gain)
+        _, kv_unit, kv_inv = norm_forward(kv_latent, kv_gain)
+        place = lax.axis_index('tp') * rows
+        cos_here = jnp.tile(lax.dynamic_slice_in_dim(rope_cos, place, rows, 0), (batch, 1))
+        sin_here = jnp.tile(lax.dynamic_slice_in_dim(rope_sin, place, rows, 0), (batch, 1))
         grad_q_lat, grad_q_gain = norm_backward(grad_lat[:, :q_rank], q_unit, q_inv, q_gain)
         grad_kv_lat, grad_kv_gain = norm_backward(grad_lat[:, q_rank:q_rank + kv_rank], kv_unit, kv_inv, kv_gain)
         gk = grad_lat[:, q_rank + kv_rank:q_rank + kv_rank + rope]

time: 599 us -> 599 us (level)
  Pallas kernels: 226 us -> 240 us
  waiting for transfers between devices: 238 us -> 229 us
  other arithmetic: 36.1 us -> 28.8 us
    pallas_call x0 -> x2, Pallas kernels: none -> 49.5 us  [the longest x1 39.1 us: local_step(): pl.pallas_call(functools.partial(weights_kernel, q_rank, kv_rank), grid=(...]
    pallas_call x1, Pallas kernels: 138 us -> 103 us  [local_step(): pl.pallas_call(functools.partial(backward_kernel, dims, score_scale, head...]
    all_gather x1, waiting for transfers between devices: 32.6 us -> 0.01 us  [local_step(): gathered = lax.all_gather(packed, 'tp', axis=0)]
    reduce_scatter x1, waiting for transfers between devices: 59.8 us -> 84.2 us  [local_step(): lax.psum_scatter(attn_part, 'tp', scatter_dimension=0, tiled=False)]
    convert_element_type x9 -> x4, other arithmetic: 11.2 us -> 2.74 us  [the longest x1 1.58 us: local_step(): grad_lat = grad_lat.reshape(here, lat_width).astype(F32)]
    dot_general x7 -> x5, matrix products: 44.9 us -> 46.2 us  [dot(): lax.dot_general(lhs, rhs, (((lhs_dim,), (rhs_dim,)), ((), ())), preferred...]
  transfers between devices with their start and end apart: 6 -> 6, of which waited for: 6 -> 5; matrix products, arithmetic and copies ran while one was open for 12% -> 15% of each run, Pallas kernels for 15% -> 21%
where the time goes in v2:
time: 599 us; the launch traced here: 597 us
  Pallas kernels  240 us (40%)
  waiting for transfers between devices  229 us (38%)
  matrix products  46.2 us (8%)
  local copies, waits for them, and re-layouts  38.2 us (6%)
  other arithmetic  28.8 us (5%)
  between operations  14.5 us (2%)
    pallas_call x1, Pallas kernels, local_step(): pl.pallas_call(functools.partial(backward_kernel, dims, score_scale, head...  103 us
    pallas_call x1, Pallas kernels, local_step(): pl.pallas_call(functools.partial(forward_kernel, dims, score_scale, heads...  87.6 us
    reduce_scatter x1, waiting for transfers between devices, local_step(): lax.psum_scatter(attn_part, 'tp', scatter_dimension=0, tiled=False)  84.2 us
    all_gather x1, waiting for transfers between devices, local_step(): lat_all = lax.all_gather(lat_here, 'tp', axis=0)  52.6 us
    reduce_scatter x1, waiting for transfers between devices, local_step(): grad_lat = lax.psum_scatter(glat, 'tp', scatter_dimension=0, tiled=False)  49.8 us
    dot_general x5, matrix products, dot(): lax.dot_general(lhs, rhs, (((lhs_dim,), (rhs_dim,)), ((), ())), preferred...  46.2 us
    pallas_call x1, Pallas kernels, local_step(): pl.pallas_call(functools.partial(weights_kernel, q_rank, kv_rank), grid=(...  39.1 us
    reduce_scatter x1, waiting for transfers between devices, local_step(): lax.psum_scatter(jnp.concatenate([part_dq, part_dkv], axis=1), 'tp', scat...  27 us
  transfers between devices with their start and end apart: 6, of which 5 were waited for; matrix products, arithmetic and copies ran while one was open for 15% of the time, Pallas kernels for 21%

profile of v2, /device:TPU:81, one launch (start us, length us, event | category | flops | bytes accessed | tf_op | source)
XLA Modules:
  0.0 596.8 jit_solution(3527674181883848219)
XLA Ops:
  7.3 0.7 neg.3
  8.0 0.8 copy.50
  8.8 1.3 broadcast_in_dim.10.gain_ref
  10.1 1.3 broadcast_in_dim.11.qgain_ref
  11.4 1.2 broadcast_in_dim.12.kvgain_ref
  12.6 0.8 copy.47
  13.4 0.1 copy.49
  13.5 1.0 concatenate.19.tab_ref
  14.5 10.5 %latents.1 = (bf16[512,2560]{1,0:T(8,128)(2,1)}, bf16[512,768]{1,0:T(8,128)(2,1)}, bf16[512,256]{1,0:T(8,128)(2,1)}, bf16[16,32,1152]{2,1,0:T(8,128)(2,1)}) custom-call(bf16[16,32,2560]{2,1,0:T(8,128)(2,1)} %x_ref.1, bf16[1,2560]{1,0:T(2,128)(2,1)} %broadcast_in_dim.10.gain_ref, bf16[2560,768]{1,0:T(8,128)(2,1)} %wdq_ref.1, bf16[288,2560]{1,0:T(8,128)(2,1)} %bitcast.96, ...), custom_call_target="tpu_custom_call" | custom-call | flops 2768240640 | bytes 12000000 | tf_op jit(solution)/shard_map/latents/pallas_call | solution.py:311
  25.1 0.1 all-gather.10.cloned.1.call-start
  25.1 0.7 all-gather.10.cloned.1.call-update
  26.0 0.5 copy-done.10
  26.4 0.2 copy-done.13
  26.6 1.6 pad_maximum_fusion.1
  28.2 52.6 %all-gather.8.cloned.1.call-done = bf16[128,32,1152]{2,1,0:T(8,128)(2,1)} async-done(((bf16[16,32,1152]{2,1,0:T(8,128)(2,1)}), bf16[128,32,1152]{2,1,0:T(8,128)(2,1)}) %all-gather.8.cloned.1.call-update) | async-done | bytes 9437200 | tf_op jit(solution)/shard_map/all_gather | solution.py:322
  80.8 87.6 %attn_forward.1 = (bf16[16,1536,256]{2,1,0:T(8,128)(2,1)}, bf16[8,16,32,1024]{3,2,1,0:T(8,128)(2,1)}, f32[16,16,256]{2,1,0:T(8,128)}, bf16[8,16,32,2560]{3,2,1,0:T(8,128)(2,1)}) custom-call(bf16[8,16,32,1152]{3,2,1,0:T(8,128)(2,1)} %bitcast.106, bf16[1536,768]{1,0:T(8,128)(2,1)} %bitcast.93, bf16[1024,256]{1,0:T(8,128)(2,1)} %bitcast.111, ...), custom_call_target="tpu_custom_call" | custom-call | flops 44023414784 | bytes 70000000 | tf_op jit(solution)/shard_map/attn_forward/pallas_call | solution.py:348
  168.4 13.6 %all-gather.10.cloned.1.call-done = bf16[128,32,2560]{2,1,0:T(8,128)(2,1)} async-done(((bf16[16,32,2560]{2,1,0:T(8,128)(2,1)}), bf16[128,32,2560]{2,1,0:T(8,128)(2,1)}) %all-gather.10.cloned.1.call-update) | async-done | bytes 20971536 | tf_op jit(solution)/shard_map/all_gather | solution.py:323
  182.0 102.8 %attn_backward.1 = (bf16[8,16,32,1152]{3,2,1,0:T(8,128)(2,1)}, bf16[16,1536,256]{2,1,0:T(8,128)(2,1)}, bf16[16,1024,256]{2,1,0:T(8,128)(2,1)}, bf16[16,1024,256]{2,1,0:T(8,128)(2,1)}) custom-call(bf16[8,16,32,1152]{3,2,1,0:T(8,128)(2,1)} %bitcast.107, bf16[8,16,32,2560]{3,2,1,0:T(8,128)(2,1)} %bitcast.104, bf16[16,1536,256]{2,1,0:T(8,128)(2,1)} %get-tuple-element.30.q_ref, ...), custom_call_target="tpu_custom_call" | custom-call | flops 75161927680 | bytes 60000000 | tf_op jit(solution)/shard_map/attn_backward/pallas_call | solution.py:362
  285.0 0.5 reduce-scatter.4.cloned.1.call-update
  285.5 0.2 reduce-scatter.8.cloned.1.call-start
  285.7 0.6 convert_element_type.87
  286.3 0.6 convert_element_type.90
  286.9 0.1 constant_dynamic-slice_fusion
  287.0 0.1 copy.52
  287.0 0.7 copy.51
  287.7 0.1 fusion.18
  287.9 0.2 fusion.9
  288.1 0.6 add_rsqrt_fusion.2
  288.7 0.6 add_rsqrt_fusion.1
  289.3 49.8 %reduce-scatter.6.cloned.1.call-done = bf16[1,16,32,1152]{3,2,1,0:T(8,128)(2,1)} async-done(((bf16[8,16,32,1152]{3,2,1,0:T(8,128)(2,1)}), bf16[1,16,32,1152]{3,2,1,0:T(8,128)(2,1)}) %reduce-scatter.6.cloned.1.call-update) | async-done | bytes 1179664 | tf_op jit(solution)/shard_map/reduce_scatter | solution.py:373
  339.1 1.6 convert.20
  340.8 0.1 fusion.20
  340.9 1.0 fusion.17
  342.0 1.2 fusion.16
  343.2 2.1 convolution_convert_fusion.1
  345.3 4.0 reshape.151
  349.3 0.5 fusion.8
  349.9 4.3 convolution_convert_fusion
  354.2 2.8 pad_maximum_fusion
  357.0 0.1 all-gather.12.cloned.1.call-start
  357.1 0.6 copy-done.17
  357.7 7.6 %fusion.28 = f32[512,2560]{1,0:T(8,128)} fusion(bf16[2560,768]{1,0:T(8,128)(2,1)} %wdq_ref.1, bf16[512,768]{1,0:T(8,128)(2,1)S(1)} %copy-done.5, f32[512,1152]{1,0:T(8,128)} %copy-done.1, f32[512]{0:T(512)} %copy-done.24, f32[768]{0:T(1024)} %convert_element_type.87, f32[512]{0:T(512)} %add_rsqrt_fusion.2), kind=kOutput, calls=%fused_computation.72 | convolution fusion | flops 2016018432 | bytes 11542528 | tf_op jit(solution)/shard_map/dot_general | solution.py:35
  365.3 84.2 %reduce-scatter.4.cloned.1.call-done = bf16[1,16,32,2560]{3,2,1,0:T(8,128)(2,1)} async-done(((bf16[8,16,32,2560]{3,2,1,0:T(8,128)(2,1)}), bf16[1,16,32,2560]{3,2,1,0:T(8,128)(2,1)}) %reduce-scatter.4.cloned.1.call-update) | async-done | bytes 2621456 | tf_op jit(solution)/shard_map/reduce_scatter | solution.py:359
  449.5 4.5 multiply_reduce_fusion.2
  454.0 0.1 rsqrt.28
  454.1 6.0 multiply_reduce_fusion
  460.1 27.0 %reduce-scatter.8.cloned.1.call-done = bf16[1,440,768]{2,1,0:T(8,128)(2,1)} async-done(((bf16[8,440,768]{2,1,0:T(8,128)(2,1)}), bf16[1,440,768]{2,1,0:T(8,128)(2,1)}) %reduce-scatter.8.cloned.1.call-update) | async-done | bytes 675856 | tf_op jit(solution)/shard_map/reduce_scatter | solution.py:409
  487.2 2.0 maximum_bitcast_fusion
  489.2 12.0 %copy.53 = bf16[1024,4096]{1,0:T(8,128)(2,1)} copy(bf16[1024,4096]{0,1:T(8,128)(2,1)} %bitcast.86) | data formatting | bytes 16777216 | tf_op jit(solution)/shard_map/dot_general | solution.py:35
  501.2 39.1 %head_weight_grads.1 = (f32[1536,768]{1,0:T(8,128)}, f32[1024,256]{1,0:T(8,128)}, f32[1024,256]{1,0:T(8,128)}) custom-call(bf16[8,16,32,1152]{3,2,1,0:T(8,128)(2,1)} %bitcast.108, bf16[16,1536,256]{2,1,0:T(8,128)(2,1)} %get-tuple-element.35.dq_ref, bf16[16,1024,256]{2,1,0:T(8,128)(2,1)} %get-tuple-element.36.dk_ref, ...), custom_call_target="tpu_custom_call" | custom-call | flops 13958643712 | bytes 50000000 | tf_op jit(solution)/shard_map/head_weight_grads/pallas_call | solution.py:376
  540.3 2.9 slice_bitcast_fusion.1
  543.1 4.4 slice_bitcast_fusion
  547.6 26.2 %fusion.30 = f32[16,64,2560]{2,1,0:T(8,128)} fusion(bf16[16,64,4096]{2,1,0:T(8,128)(2,1)S(1)} %bitcast.87, bf16[4096,2560,1]{1,0,2:T(8,128)(2,1)} %bitcast.105), kind=kOutput, calls=%fused_computation.73 | convolution fusion | flops 21474836480 | bytes 39845888 | tf_op jit(solution)/shard_map/dot_general | solution.py:35
  573.8 4.4 convert_add_fusion
  578.2 1.0 slice_convert_fusion.1
  579.2 0.2 reshape.165
  579.4 0.3 fusion.23
  579.7 0.6 slice.71
  580.3 0.6 slice.73
  580.9 0.6 slice.75
  581.5 2.1 slice-done.4
  583.6 4.1 bitcast_convert_fusion
  587.7 0.2 slice_convert_fusion
  587.9 2.0 reshape.167
  (78 shorter events, 0.6 us)
Async XLA Ops:
  7.2 73.6 %all-gather.8.cloned.1.call-start = ((), (), s32[]{:S(2)}) async-start(), calls=%async_computation.6 | async-start | bytes 10616832 | tf_op jit(solution)/shard_map/all_gather | solution.py:322
  25.0 1.4 copy-start.10
  25.0 1.6 copy-start.13
  25.1 156.9 %all-gather.10.cloned.1.call-start = ((), (), s32[]{:S(2)}) async-start(), calls=%async_computation.7 | async-start | bytes 23592960 | tf_op jit(solution)/shard_map/all_gather | solution.py:323
  25.9 313.3 %reduce-scatter.6.cloned.1.call-start = ((), (), s32[]{:S(2)}) async-start(), calls=%async_computation.4 | async-start | bytes 10616832 | tf_op jit(solution)/shard_map/reduce_scatter | solution.py:373
  284.8 164.7 %reduce-scatter.4.cloned.1.call-start = ((), (), s32[]{:S(2)}) async-start(), calls=%async_computation.3 | async-start | bytes 23592960 | tf_op jit(solution)/shard_map/reduce_scatter | solution.py:359
  284.9 0.8 copy-start.21
  284.9 1.4 copy-start.25
  284.9 2.0 copy-start.14
  284.9 2.0 copy-start.16
  284.9 2.8 copy-start.9
  285.0 2.9 copy-start.5
  285.5 201.7 %reduce-scatter.8.cloned.1.call-start = ((), (), s32[]{:S(2)}) async-start(), calls=%async_computation.5 | async-start | bytes 6082560 | tf_op jit(solution)/shard_map/reduce_scatter | solution.py:409
  339.1 1.6 copy-start.15
  339.1 1.8 copy-start.18
  339.1 1.8 copy-start.22
  339.1 4.0 copy-start.6
  340.7 9.1 %copy-start.1 = (f32[512,1152]{1,0:T(8,128)}, f32[512,1152]{1,0:T(8,128)S(1)}, u32[]{:S(2)}) copy-start(f32[512,1152]{1,0:T(8,128)S(1)} %convert.20) | copy-start | bytes 7077892
  340.9 2.2 copy-start.11
  343.2 6.2 %copy-start.7 = (bf16[512,256]{1,0:T(8,128)(2,1)}, bf16[512,256]{1,0:T(8,128)(2,1)S(1)}, u32[]{:S(2)}) copy-start(bf16[512,256]{1,0:T(8,128)(2,1)S(1)} %fusion.16) | copy-start | bytes 786436
  343.2 6.1 %copy-start.19 = (f32[768]{0:T(1024)S(1)}, f32[768]{0:T(1024)}, u32[]{:S(2)}) copy-start(f32[768]{0:T(1024)} %convert_element_type.87) | copy-start | bytes 9220
  343.2 6.1 %copy-start.20 = (f32[512]{0:T(512)S(1)}, f32[512]{0:T(512)}, u32[]{:S(2)}) copy-start(f32[512]{0:T(512)} %add_rsqrt_fusion.2) | copy-start | bytes 6148
  349.9 4.3 copy-start.24
  349.9 4.3 copy-start.4
  357.0 0.7 copy-start.17
  357.0 221.2 %all-gather.12.cloned.1.call-start = ((), (), s32[]{:S(2)}) async-start(), calls=%async_computation.8 | async-start | bytes 6303744 | tf_op jit(solution)/shard_map/all_gather | solution.py:421
  357.6 91.8 %copy-start = (bf16[16,32,2560]{2,1,0:T(8,128)(2,1)S(1)}, bf16[16,32,2560]{2,1,0:T(8,128)(2,1)}, u32[]{:S(2)}) copy-start(bf16[16,32,2560]{2,1,0:T(8,128)(2,1)} %x_ref.1) | copy-start | bytes 7864324
  365.3 88.9 %copy-start.8 = (bf16[512,256]{1,0:T(8,128)(2,1)S(1)}, bf16[512,256]{1,0:T(8,128)(2,1)}, u32[]{:S(2)}) copy-start(bf16[512,256]{1,0:T(8,128)(2,1)} %copy-done.7) | copy-start | bytes 786436
  365.3 88.9 %copy-start.12 = (bf16[512,16]{1,0:T(8,128)(2,1)S(1)}, bf16[512,16]{1,0:T(8,128)(2,1)}, u32[]{:S(2)}) copy-start(bf16[512,16]{1,0:T(8,128)(2,1)} %copy-done.11) | copy-start | bytes 49156
  454.1 6.0 copy-start.23
  540.3 7.3 %copy-start.3 = (bf16[1024,4096]{1,0:T(8,128)(2,1)S(1)}, bf16[1024,4096]{1,0:T(8,128)(2,1)}, u32[]{:S(2)}) copy-start(bf16[1024,4096]{1,0:T(8,128)(2,1)} %copy.53) | copy-start | bytes 25165828
  547.6 26.3 %slice-start = ((s8[5242880]{0:T(1024)(128)(4,1)}), s8[4194304]{0:T(1024)(128)(4,1)S(1)}, s32[]{:S(2)}) async-start(s8[5242880]{0:T(1024)(128)(4,1)} %bitcast.82), calls=%async_computation.9 | async-start | bytes 8388608
  547.6 26.2 %slice-start.1 = ((s8[5242880]{0:T(1024)(128)(4,1)}), s8[1048576]{0:T(1024)(128)(4,1)S(1)}, s32[]{:S(2)}) async-start(s8[5242880]{0:T(1024)(128)(4,1)} %bitcast.82), calls=%async_computation.10 | async-start | bytes 2097152
  547.6 26.3 %copy-start.2 = (bf16[16,32,2560]{2,1,0:T(8,128)(2,1)S(1)}, bf16[16,32,2560]{2,1,0:T(8,128)(2,1)}, u32[]{:S(2)}) copy-start(bf16[16,32,2560]{2,1,0:T(8,128)(2,1)} %param.27) | copy-start | bytes 7864324
  581.5 2.1 slice-start.4
  581.5 6.2 %slice-start.2 = ((s8[5603328]{0:T(1024)(128)(4,1)}), s8[4194304]{0:T(1024)(128)(4,1)S(1)}, s32[]{:S(2)}) async-start(s8[5603328]{0:T(1024)(128)(4,1)} %bitcast.84), calls=%async_computation.11 | async-start | bytes 8388608
  583.6 4.1 slice-start.3
Sparse Core Ops, SparseCore 0:
  25.2 55.5 all-gather.7
  82.3 99.6 all-gather.9
  284.9 54.1 reduce-scatter.5
  341.4 108.0 reduce-scatter.3
  452.2 34.8 reduce-scatter.7
  489.3 37.1 all-gather.11

commit v3 on v2

--- a/solution.py
+++ b/solution.py
@@ -227,27 +227,22 @@
     glat_ref[:, 0, :, q_rank + kv_rank:] = jnp.transpose(padded).astype(BF16).reshape(shards, rows, 128)
 
 
-def weights_kernel(q_rank, kv_rank, lat_ref, dq_ref, dk_ref, dv_ref, gwq_ref, gwk_ref, gwv_ref):
-    shards, _, rows, _ = lat_ref.shape
+def weights_kernel(first, width, lat_ref, *refs):
+    shards, batch, rows, _ = lat_ref.shape
     seq = shards * rows
-    q_lat = lat_ref[:, 0, :, :q_rank].reshape(seq, q_rank)
-    kv_lat = lat_ref[:, 0, :, q_rank:q_rank + kv_rank].reshape(seq, kv_rank)
-    step = 256
+    count = len(refs) // 2
 
     @pl.when(pl.program_id(0) == 0)
     def _():
-        gwq_ref[...] = jnp.zeros_like(gwq_ref)
-        gwk_ref[...] = jnp.zeros_like(gwk_ref)
-        gwv_ref[...] = jnp.zeros_like(gwv_ref)
-
-    def q_step(i, carry):
-        at = pl.ds(pl.multiple_of(i * step, step), step)
-        gwq_ref[at, :] += dot(dq_ref[0, at, :], q_lat, 1, 0)
-        return carry
-
-    lax.fori_loop(0, gwq_ref.shape[0] // step, q_step, 0)
-    gwk_ref[...] += dot(dk_ref[0], kv_lat, 1, 0)
-    gwv_ref[...] += dot(dv_ref[0], kv_lat, 1, 0)
+        for out_ref in refs[count:]:
+            out_ref[...] = jnp.zeros_like(out_ref)
+
+    step = 512
+    lats = [lat_ref[:, j, :, first:first + width].reshape(seq, width) for j in range(batch)]
+    for grad_ref, out_ref in zip(refs[:count], refs[count:]):
+        for i in range(0, out_ref.shape[0], step):
+            at = pl.ds(i, step)
+            out_ref[at, :] += sum(dot(grad_ref[j, at, :], lats[j], 1, 0) for j in range(batch))
 
 
 def latent_kernel(axis, x_ref, gain_ref, wdq_ref, wdkv_ref, qgain_ref, kvgain_ref, tab_ref, normed_ref, qlat_ref, kvlat_ref, lat_ref, wr_buf):
@@ -373,21 +368,24 @@
         grad_lat = lax.psum_scatter(glat, 'tp', scatter_dimension=0, tiled=False)
         grad_lat = grad_lat.reshape(here, lat_width).astype(F32)
 
-        gwq, gwk, gwv = pl.pallas_call(
-            functools.partial(weights_kernel, q_rank, kv_rank),
-            grid=(batch,),
-            in_specs=[tok(lat_width)] + [per_batch((w.shape[0], seq)) for w in (wq, wk, wv)],
-            out_specs=[fixed(w.shape) for w in (wq, wk, wv)],
-            out_shape=[jax.ShapeDtypeStruct(w.shape, F32) for w in (wq, wk, wv)],
-            compiler_params=pltpu.CompilerParams(dimension_semantics=("arbitrary",)),
-            cost_estimate=pl.CostEstimate(flops=up_flops, bytes_accessed=50_000_000, transcendentals=0),
-            name="head_weight_grads",
-        )(lat_all, dq_all, dk_all, dv_all)
+        many = 4 if batch % 4 == 0 else 1
+
+        def weight_grads(first, width, grads):
+            shapes = [(g.shape[1], width) for g in grads]
+            return pl.pallas_call(
+                functools.partial(weights_kernel, first, width),
+                grid=(batch // many,),
+                in_specs=[pl.BlockSpec((shards, many, rows, lat_width), lambda b: (0, b, 0, 0))] + [pl.BlockSpec((many,) + g.shape[1:], lambda b: (b, 0, 0)) for g in grads],
+                out_specs=[fixed(shape) for shape in shapes],
+                out_shape=[jax.ShapeDtypeStruct(shape, F32) for shape in shapes],
+                compiler_params=pltpu.CompilerParams(dimension_semantics=("arbitrary",)),
+                cost_estimate=pl.CostEstimate(flops=2 * tokens * width * sum(shape[0] for shape in shapes), bytes_accessed=30_000_000, transcendentals=0),
+            )(lat_all, *grads)
+
+        gwq, = weight_grads(0, q_rank, [dq_all])
         grad_wq = gwq.reshape(heads, nope + rope, q_rank)
         grad_w_uq = grad_wq[:, :nope].transpose(2, 0, 1)
         grad_w_qr = grad_wq[:, nope:].transpose(2, 0, 1)
-        grad_w_uk = gwk.reshape(heads, nope, kv_rank).transpose(2, 0, 1)
-        grad_w_uv = gwv.reshape(heads, value, kv_rank).transpose(2, 0, 1)
         grad_w_out = dot(o_all.reshape(tokens, heads * value), dy_all.reshape(tokens, dim), 0, 0).reshape(heads, value, dim)
 
         _, x_unit, x_inv = norm_forward(x2, norm_gain)
@@ -406,7 +404,11 @@
         own_kv = kv_width // shards * dim // q_rank
         part_dq = dot(normed, grad_q_lat, 0, 0).astype(BF16).reshape(shards, own, q_rank)
         part_dkv = dot(grad_kv_all, normed, 0, 0).astype(BF16).reshape(shards, own_kv, q_rank)
-        down_sum = lax.psum_scatter(jnp.concatenate([part_dq, part_dkv], axis=1), 'tp', scatter_dimension=0, tiled=False)
+        down_part, dk_all, dv_all = lax.optimization_barrier((jnp.concatenate([part_dq, part_dkv], axis=1), dk_all, dv_all))
+        down_sum = lax.psum_scatter(down_part, 'tp', scatter_dimension=0, tiled=False)
+        gwk, gwv = weight_grads(q_rank, kv_rank, [dk_all, dv_all])
+        grad_w_uk = gwk.reshape(heads, nope, kv_rank).transpose(2, 0, 1)
+        grad_w_uv = gwv.reshape(heads, value, kv_rank).transpose(2, 0, 1)
         grad_normed = dot(grad_q_lat, w_dq, 1, 1) + dot(grad_kv_all, w_dkv, 1, 1)
         grad_x_norm, grad_norm_gain = norm_backward(grad_normed, x_unit, x_inv, norm_gain)
         grad_hidden = grad_out.reshape(here, dim).astype(F32) + grad_x_norm

time: 599 us -> 590 us (0.985)
  Pallas kernels: 240 us -> 228 us
    pallas_call x1 -> x2, Pallas kernels: 39.1 us -> 27.3 us  [weight_grads(): pl.pallas_call(functools.partial(weights_kernel, first, width), grid=(bat...]
  transfers between devices with their start and end apart: 6 -> 6, of which waited for: 5 -> 5; matrix products, arithmetic and copies ran while one was open for 15% -> 16% of each run, Pallas kernels for 21% -> 20%
where the time goes in v3:
time: 590 us; the launch traced here: 588 us
  waiting for transfers between devices  229 us (39%)
  Pallas kernels  228 us (39%)
  matrix products  45.9 us (8%)
  local copies, waits for them, and re-layouts  38.4 us (7%)
  other arithmetic  31.6 us (5%)
  between operations  14.5 us (2%)
    pallas_call x1, Pallas kernels, local_step(): pl.pallas_call(functools.partial(backward_kernel, dims, score_scale, head...  103 us
    pallas_call x1, Pallas kernels, local_step(): pl.pallas_call(functools.partial(forward_kernel, dims, score_scale, heads...  87.5 us
    reduce_scatter x1, waiting for transfers between devices, local_step(): lax.psum_scatter(attn_part, 'tp', scatter_dimension=0, tiled=False)  84.2 us
    all_gather x1, waiting for transfers between devices, local_step(): lat_all = lax.all_gather(lat_here, 'tp', axis=0)  52.6 us
    reduce_scatter x1, waiting for transfers between devices, local_step(): grad_lat = lax.psum_scatter(glat, 'tp', scatter_dimension=0, tiled=False)  49.9 us
    dot_general x5, matrix products, dot(): lax.dot_general(lhs, rhs, (((lhs_dim,), (rhs_dim,)), ((), ())), preferred...  45.9 us
    pallas_call x2, Pallas kernels, weight_grads(): pl.pallas_call(functools.partial(weights_kernel, first, width), grid=(bat...  27.3 us
    reduce_scatter x1, waiting for transfers between devices, local_step(): lax.psum_scatter(down_part, 'tp', scatter_dimension=0, tiled=False)  27 us
  transfers between devices with their start and end apart: 6, of which 5 were waited for; matrix products, arithmetic and copies ran while one was open for 16% of the time, Pallas kernels for 20%

profile of v3, /device:TPU:81, one launch (start us, length us, event | category | flops | bytes accessed | tf_op | source)
XLA Modules:
  0.0 587.9 jit_solution(5299561722726055585)
XLA Ops:
  7.3 0.7 neg.3
  8.0 0.8 copy.50
  8.8 1.3 broadcast_in_dim.10.gain_ref
  10.1 1.3 broadcast_in_dim.11.qgain_ref
  11.4 1.2 broadcast_in_dim.12.kvgain_ref
  12.6 0.8 copy.47
  13.4 0.1 copy.49
  13.5 1.0 concatenate.19.tab_ref
  14.5 10.5 %latents.1 = (bf16[512,2560]{1,0:T(8,128)(2,1)}, bf16[512,768]{1,0:T(8,128)(2,1)}, bf16[512,256]{1,0:T(8,128)(2,1)}, bf16[16,32,1152]{2,1,0:T(8,128)(2,1)}) custom-call(bf16[16,32,2560]{2,1,0:T(8,128)(2,1)} %x_ref.1, bf16[1,2560]{1,0:T(2,128)(2,1)} %broadcast_in_dim.10.gain_ref, bf16[2560,768]{1,0:T(8,128)(2,1)} %wdq_ref.1, bf16[288,2560]{1,0:T(8,128)(2,1)} %bitcast.98, ...), custom_call_target="tpu_custom_call" | custom-call | flops 2768240640 | bytes 12000000 | tf_op jit(solution)/shard_map/latents/pallas_call | solution.py:306
  25.1 0.7 all-gather.10.cloned.1.call-update
  26.0 0.5 copy-done.9
  26.4 0.2 copy-done.12
  26.6 1.6 pad_maximum_fusion.1
  28.2 52.6 %all-gather.8.cloned.1.call-done = bf16[128,32,1152]{2,1,0:T(8,128)(2,1)} async-done(((bf16[16,32,1152]{2,1,0:T(8,128)(2,1)}), bf16[128,32,1152]{2,1,0:T(8,128)(2,1)}) %all-gather.8.cloned.1.call-update) | async-done | bytes 9437200 | tf_op jit(solution)/shard_map/all_gather | solution.py:317
  80.8 87.5 %attn_forward.1 = (bf16[16,1536,256]{2,1,0:T(8,128)(2,1)}, bf16[8,16,32,1024]{3,2,1,0:T(8,128)(2,1)}, f32[16,16,256]{2,1,0:T(8,128)}, bf16[8,16,32,2560]{3,2,1,0:T(8,128)(2,1)}) custom-call(bf16[8,16,32,1152]{3,2,1,0:T(8,128)(2,1)} %bitcast.84, bf16[1536,768]{1,0:T(8,128)(2,1)} %bitcast.95, bf16[1024,256]{1,0:T(8,128)(2,1)} %bitcast.112, ...), custom_call_target="tpu_custom_call" | custom-call | flops 44023414784 | bytes 70000000 | tf_op jit(solution)/shard_map/attn_forward/pallas_call | solution.py:343
  168.3 13.7 %all-gather.10.cloned.1.call-done = bf16[128,32,2560]{2,1,0:T(8,128)(2,1)} async-done(((bf16[16,32,2560]{2,1,0:T(8,128)(2,1)}), bf16[128,32,2560]{2,1,0:T(8,128)(2,1)}) %all-gather.10.cloned.1.call-update) | async-done | bytes 20971536 | tf_op jit(solution)/shard_map/all_gather | solution.py:318
  182.0 102.8 %attn_backward.1 = (bf16[8,16,32,1152]{3,2,1,0:T(8,128)(2,1)}, bf16[16,1536,256]{2,1,0:T(8,128)(2,1)}, bf16[16,1024,256]{2,1,0:T(8,128)(2,1)}, bf16[16,1024,256]{2,1,0:T(8,128)(2,1)}) custom-call(bf16[8,16,32,1152]{3,2,1,0:T(8,128)(2,1)} %bitcast.85, bf16[8,16,32,2560]{3,2,1,0:T(8,128)(2,1)} %bitcast.106, bf16[16,1536,256]{2,1,0:T(8,128)(2,1)} %get-tuple-element.32.q_ref, ...), custom_call_target="tpu_custom_call" | custom-call | flops 75161927680 | bytes 60000000 | tf_op jit(solution)/shard_map/attn_backward/pallas_call | solution.py:357
  285.0 0.5 reduce-scatter.4.cloned.1.call-update
  285.5 0.2 reduce-scatter.8.cloned.1.call-start
  285.7 0.6 convert_element_type.87
  286.3 0.6 convert_element_type.90
  286.9 0.1 constant_dynamic-slice_fusion
  287.0 0.1 copy.52
  287.1 0.7 copy.51
  287.7 0.1 fusion.18
  287.9 0.2 fusion.9
  288.1 0.6 add_rsqrt_fusion.2
  288.7 0.6 add_rsqrt_fusion.1
  289.3 49.9 %reduce-scatter.6.cloned.1.call-done = bf16[1,16,32,1152]{3,2,1,0:T(8,128)(2,1)} async-done(((bf16[8,16,32,1152]{3,2,1,0:T(8,128)(2,1)}), bf16[1,16,32,1152]{3,2,1,0:T(8,128)(2,1)}) %reduce-scatter.6.cloned.1.call-update) | async-done | bytes 1179664 | tf_op jit(solution)/shard_map/reduce_scatter | solution.py:368
  339.2 1.6 convert.20
  340.8 0.1 fusion.20
  341.0 1.0 fusion.17
  342.0 1.2 fusion.16
  343.2 2.1 convolution_convert_fusion.1
  345.3 4.0 reshape.151
  349.4 0.5 fusion.8
  349.9 4.3 convolution_convert_fusion
  354.2 2.8 pad_maximum_fusion
  357.1 0.1 all-gather.12.cloned.1.call-start
  357.1 0.6 copy-done.16
  357.7 7.6 %fusion.28 = f32[512,2560]{1,0:T(8,128)} fusion(bf16[2560,768]{1,0:T(8,128)(2,1)} %wdq_ref.1, bf16[512,768]{1,0:T(8,128)(2,1)S(1)} %copy-done.4, f32[512,1152]{1,0:T(8,128)} %copy-done.1, f32[512]{0:T(512)} %copy-done.23, f32[768]{0:T(1024)} %convert_element_type.87, f32[512]{0:T(512)} %add_rsqrt_fusion.2), kind=kOutput, calls=%fused_computation.72 | convolution fusion | flops 2016018432 | bytes 11542528 | tf_op jit(solution)/shard_map/dot_general | solution.py:35
  365.3 84.2 %reduce-scatter.4.cloned.1.call-done = bf16[1,16,32,2560]{3,2,1,0:T(8,128)(2,1)} async-done(((bf16[8,16,32,2560]{3,2,1,0:T(8,128)(2,1)}), bf16[1,16,32,2560]{3,2,1,0:T(8,128)(2,1)}) %reduce-scatter.4.cloned.1.call-update) | async-done | bytes 2621456 | tf_op jit(solution)/shard_map/reduce_scatter | solution.py:354
  449.5 4.5 multiply_reduce_fusion.2
  454.1 0.1 rsqrt.28
  454.2 6.0 %multiply_reduce_fusion = (f32[2560]{0:T(1024)S(1)}, f32[512]{0:T(512)S(1)}, f32[512,2560]{1,0:T(8,128)}) fusion(bf16[16,32,2560]{2,1,0:T(8,128)(2,1)S(1)} %copy-done, f32[512]{0:T(512)S(1)} %rsqrt.28, f32[2560]{0:T(1024)S(1)} %convert_element_type.91, f32[512,2560]{1,0:T(8,128)} %fusion.28, bf16[2560,288]{0,1:T(8,128)(2,1)} %param.18, ...), kind=kOutput, calls=%fused_computation.5 | convolution fusion | flops 766342144 | bytes 14901248 | tf_op jit(solution)/shard_map/dot_general | solution.py:35
  460.2 27.0 %reduce-scatter.8.cloned.1.call-done = bf16[1,440,768]{2,1,0:T(8,128)(2,1)} async-done(((bf16[8,440,768]{2,1,0:T(8,128)(2,1)}), bf16[1,440,768]{2,1,0:T(8,128)(2,1)}) %reduce-scatter.8.cloned.1.call-update) | async-done | bytes 675856 | tf_op jit(solution)/shard_map/reduce_scatter | solution.py:408
  487.2 2.0 maximum_bitcast_fusion
  489.3 12.0 %copy.53 = bf16[1024,4096]{1,0:T(8,128)(2,1)} copy(bf16[1024,4096]{0,1:T(8,128)(2,1)} %bitcast.88) | data formatting | bytes 16777216 | tf_op jit(solution)/shard_map/dot_general | solution.py:35
  501.3 15.7 %shard_map.229 = f32[1536,768]{1,0:T(8,128)} custom-call(bf16[8,16,32,1152]{3,2,1,0:T(8,128)(2,1)} %bitcast.86, bf16[16,1536,256]{2,1,0:T(8,128)(2,1)} %get-tuple-element.40.refs_0_), custom_call_target="tpu_custom_call" | custom-call | flops 9663676416 | bytes 30000000 | tf_op jit(solution)/shard_map/pallas_call | solution.py:375
  517.0 2.9 slice_bitcast_fusion.1
  519.9 4.5 slice_bitcast_fusion
  524.5 26.0 %fusion.30 = f32[16,64,2560]{2,1,0:T(8,128)} fusion(bf16[16,64,4096]{2,1,0:T(8,128)(2,1)S(1)} %bitcast.89, bf16[4096,2560,1]{1,0,2:T(8,128)(2,1)} %bitcast.107), kind=kOutput, calls=%fused_computation.73 | convolution fusion | flops 21474836480 | bytes 39845888 | tf_op jit(solution)/shard_map/dot_general | solution.py:35
  550.5 11.6 %shard_map.230 = (f32[1024,256]{1,0:T(8,128)}, f32[1024,256]{1,0:T(8,128)}) custom-call(bf16[8,16,32,1152]{3,2,1,0:T(8,128)(2,1)} %bitcast.87, bf16[16,1024,256]{2,1,0:T(8,128)(2,1)} %get-tuple-element.41.refs_0_, bf16[16,1024,256]{2,1,0:T(8,128)(2,1)} %get-tuple-element.42.refs_1_), custom_call_target="tpu_custom_call" | custom-call | flops 4294967296 | bytes 30000000 | tf_op jit(solution)/shard_map/pallas_call | solution.py:375
  562.1 7.3 %convert_add_fusion = f32[512,2560]{1,0:T(8,128)} fusion(f32[512,2560]{1,0:T(8,128)} %get-tuple-element.59, bf16[16,32,2560]{2,1,0:T(8,128)(2,1)S(1)} %copy-done, bf16[16,32,2560]{2,1,0:T(8,128)(2,1)} %param.27, f32[512]{0:T(512)S(1)} %broadcast_multiply_fusion, f32[2560]{0:T(1024)S(1)} %convert_element_type.91, f32[512]{0:T(512)S(1)} %rsqrt.28), kind=kLoop, calls=%fused_computation.1 | loop fusion | flops 10485760 | bytes 15742976 | tf_op jit(solution)/shard_map/add | solution.py:414
  569.4 1.0 slice_convert_fusion.1
  570.3 0.2 reshape.165
  570.5 0.3 fusion.23
  570.8 0.6 slice.71
  571.4 0.6 slice.73
  572.0 0.6 slice.75
  572.6 2.1 slice-done.2
  574.7 4.1 bitcast_convert_fusion
  578.8 0.2 slice_convert_fusion
  579.0 2.0 reshape.167
  (72 shorter events, 0.7 us)
Async XLA Ops:
  7.2 73.6 %all-gather.8.cloned.1.call-start = ((), (), s32[]{:S(2)}) async-start(), calls=%async_computation.6 | async-start | bytes 10616832 | tf_op jit(solution)/shard_map/all_gather | solution.py:317
  25.0 1.4 copy-start.9
  25.0 1.6 copy-start.12
  25.1 156.9 %all-gather.10.cloned.1.call-start = ((), (), s32[]{:S(2)}) async-start(), calls=%async_computation.7 | async-start | bytes 23592960 | tf_op jit(solution)/shard_map/all_gather | solution.py:318
  25.9 313.3 %reduce-scatter.6.cloned.1.call-start = ((), (), s32[]{:S(2)}) async-start(), calls=%async_computation.4 | async-start | bytes 10616832 | tf_op jit(solution)/shard_map/reduce_scatter | solution.py:368
  284.8 164.7 %reduce-scatter.4.cloned.1.call-start = ((), (), s32[]{:S(2)}) async-start(), calls=%async_computation.3 | async-start | bytes 23592960 | tf_op jit(solution)/shard_map/reduce_scatter | solution.py:354
  284.9 0.8 copy-start.20
  284.9 1.4 copy-start.24
  284.9 2.0 copy-start.13
  284.9 2.0 copy-start.15
  285.0 2.8 copy-start.8
  285.0 2.9 copy-start.4
  285.5 201.7 %reduce-scatter.8.cloned.1.call-start = ((), (), s32[]{:S(2)}) async-start(), calls=%async_computation.5 | async-start | bytes 6082560 | tf_op jit(solution)/shard_map/reduce_scatter | solution.py:408
  339.2 1.6 copy-start.14
  339.2 1.8 copy-start.17
  339.2 1.8 copy-start.21
  339.2 4.0 copy-start.5
  340.8 9.1 %copy-start.1 = (f32[512,1152]{1,0:T(8,128)}, f32[512,1152]{1,0:T(8,128)S(1)}, u32[]{:S(2)}) copy-start(f32[512,1152]{1,0:T(8,128)S(1)} %convert.20) | copy-start | bytes 7077892
  341.0 2.2 copy-start.10
  343.2 6.2 %copy-start.6 = (bf16[512,256]{1,0:T(8,128)(2,1)}, bf16[512,256]{1,0:T(8,128)(2,1)S(1)}, u32[]{:S(2)}) copy-start(bf16[512,256]{1,0:T(8,128)(2,1)S(1)} %fusion.16) | copy-start | bytes 786436
  343.2 6.1 %copy-start.18 = (f32[768]{0:T(1024)S(1)}, f32[768]{0:T(1024)}, u32[]{:S(2)}) copy-start(f32[768]{0:T(1024)} %convert_element_type.87) | copy-start | bytes 9220
  343.2 6.1 %copy-start.19 = (f32[512]{0:T(512)S(1)}, f32[512]{0:T(512)}, u32[]{:S(2)}) copy-start(f32[512]{0:T(512)} %add_rsqrt_fusion.2) | copy-start | bytes 6148
  349.9 4.3 copy-start.23
  349.9 4.3 copy-start.3
  357.0 0.7 copy-start.16
  357.1 212.3 %all-gather.12.cloned.1.call-start = ((), (), s32[]{:S(2)}) async-start(), calls=%async_computation.8 | async-start | bytes 6303744 | tf_op jit(solution)/shard_map/all_gather | solution.py:423
  357.7 91.8 %copy-start = (bf16[16,32,2560]{2,1,0:T(8,128)(2,1)S(1)}, bf16[16,32,2560]{2,1,0:T(8,128)(2,1)}, u32[]{:S(2)}) copy-start(bf16[16,32,2560]{2,1,0:T(8,128)(2,1)} %x_ref.1) | copy-start | bytes 7864324
  365.3 88.9 %copy-start.7 = (bf16[512,256]{1,0:T(8,128)(2,1)S(1)}, bf16[512,256]{1,0:T(8,128)(2,1)}, u32[]{:S(2)}) copy-start(bf16[512,256]{1,0:T(8,128)(2,1)} %copy-done.6) | copy-start | bytes 786436
  365.3 88.9 %copy-start.11 = (bf16[512,16]{1,0:T(8,128)(2,1)S(1)}, bf16[512,16]{1,0:T(8,128)(2,1)}, u32[]{:S(2)}) copy-start(bf16[512,16]{1,0:T(8,128)(2,1)} %copy-done.10) | copy-start | bytes 49156
  454.2 6.0 %copy-start.22 = (f32[256]{0:T(256)S(1)}, f32[256]{0:T(256)}, u32[]{:S(2)}) copy-start(f32[256]{0:T(256)} %get-tuple-element.50) | copy-start | bytes 3076
  517.0 7.5 %copy-start.2 = (bf16[1024,4096]{1,0:T(8,128)(2,1)S(1)}, bf16[1024,4096]{1,0:T(8,128)(2,1)}, u32[]{:S(2)}) copy-start(bf16[1024,4096]{1,0:T(8,128)(2,1)} %copy.53) | copy-start | bytes 25165828
  572.6 2.1 slice-start.2
  572.6 6.2 %slice-start = ((s8[5603328]{0:T(1024)(128)(4,1)}), s8[4194304]{0:T(1024)(128)(4,1)S(1)}, s32[]{:S(2)}) async-start(s8[5603328]{0:T(1024)(128)(4,1)} %bitcast.82), calls=%async_computation.9 | async-start | bytes 8388608
  574.7 4.1 slice-start.1
Sparse Core Ops, SparseCore 0:
  25.2 55.5 all-gather.7
  82.3 99.6 all-gather.9
  285.0 54.1 reduce-scatter.5
  341.4 108.0 reduce-scatter.3
  452.3 34.8 reduce-scatter.7
  489.4 37.2 all-gather.11
